TPU v7x, 128 devices: a whole 4x4x4 slice. The times are simulated.
128 devices in a mesh: grp: 2 (over z_hi), dev: 64 (over x, z_lo, y, core).
Axes of the slice: x: 4, y: 4, z: 4 (z_hi: 2, z_lo: 2; z = z_hi * 2 + z_lo), core: 2. Of those that a mesh axis runs over, the one named last changes fastest.
Arguments:
- inputs: bfloat16 [256, 196, 1024], P(('grp', 'dev')), may hold values from -6 to 6
- cotangent: bfloat16 [256, 196, 1024], P(('grp', 'dev')), may hold values from -24 to 24
- first_gain: float32 [1024], replicated, may hold values from 0.5 to 1.5
- first_shift: float32 [1024], replicated, may hold values from -3 to 3
- token_in: bfloat16 [512, 196], replicated, may hold values from -0.4375 to 0.4375
- token_in_bias: float32 [512], replicated, may hold values from -3 to 3
- token_out: bfloat16 [512, 196], replicated, may hold values from -0.25 to 0.25
- second_gain: float32 [1024], replicated, may hold values from 0.5 to 1.5
- second_shift: float32 [1024], replicated, may hold values from -3 to 3
- channel_in: bfloat16 [1024, 4096], replicated, may hold values from -0.1875 to 0.1875
- channel_in_bias: float32 [4096], replicated, may hold values from -3 to 3
- channel_out: bfloat16 [1024, 4096], replicated, may hold values from -0.09375 to 0.09375
Outputs:
- grad_inputs: bfloat16 [256, 196, 1024], P(('grp', 'dev'))
- grad_token_in: float32 [512, 196], P('dev')
- grad_token_out: float32 [512, 196], P('dev')
- grad_channel_in: float32 [1024, 4096], P('dev')
- grad_channel_out: float32 [1024, 4096], P('dev')
- grad_norms: float32 [5, 1024], replicated
- grad_token_in_bias: float32 [512], replicated
- grad_token_out_bias: float32 [196], replicated
- grad_channel_in_bias: float32 [4096], replicated
All inputs are finite; a program needn't handle non-finite values.
Results may differ from a plain program's by a relative error of at most 0.0066.
Values sent between devices are 32-bit elements; how exact they have to be, the bound alone decides.
A program may use at most 192 MiB of HBM per device.

v0:
```python
import math

import jax
import jax.numpy as jnp
from jax import lax
from jax.sharding import Mesh
from jax.sharding import PartitionSpec as P

DEV = ("dev_0", "dev_1", "dev_2", "dev_3")
GRP_DEV = ("grp", "dev_0", "dev_1", "dev_2", "dev_3")


epsilon = 1e-06


def cut_along(shard, dim, count):
    before, after = (shard.shape[:dim], shard.shape[dim + 1 :])
    return jnp.moveaxis(shard.reshape(*before, count, -1, *after), dim, 0)


def summed_rows(shard, chips, core, dim):
    sizes = (lax.axis_size(chips), lax.axis_size(core))
    blocks = cut_along(shard, dim, sizes[0] * sizes[1])
    inside = blocks.shape[1:]
    blocks = blocks.reshape(*sizes, *inside).swapaxes(0, 1).reshape(-1, *inside)
    blocks = lax.psum_scatter(blocks, core, scatter_dimension=0, tiled=True)
    return lax.psum_scatter(blocks, chips, scatter_dimension=0, tiled=True)[0]


def summed_on_arrival(shard, axis, dim):
    count = lax.axis_size(axis)
    blocks = lax.all_to_all(cut_along(shard, dim, count), axis, 0, 0, tiled=True)
    return jnp.sum(blocks, axis=0)


def copy_for_each(shard, axis):
    copies = jnp.broadcast_to(shard, (lax.axis_size(axis), *shard.shape))
    return lax.all_to_all(copies, axis, split_axis=0, concat_axis=0, tiled=True)


def of_everyone(shard, axis):
    everything = copy_for_each(shard, axis)
    return jnp.sum(everything, axis=0)


def together(arrays, axis):
    line, at, gathered = (jnp.concatenate([a.reshape(-1) for a in arrays]), 0, [])
    running = of_everyone(line, axis)
    for a in arrays:
        gathered.append(running[at : at + a.size].reshape(a.shape))
        at += a.size
    return tuple(gathered)


def together_2(arrays, axis):
    ends = [0]
    for a in arrays:
        ends.append(ends[-1] + a.size)
    running = lax.psum(jnp.concatenate([a.ravel() for a in arrays]), axis)
    return tuple((running[b:e].reshape(a.shape) for a, b, e in zip(arrays, ends, ends[1:])))


def norm_forward(values, gain, shift):
    centred = values - jnp.mean(values, axis=-1, keepdims=True)
    variance = jnp.mean(centred * centred, axis=-1, keepdims=True)
    inv_std = lax.rsqrt(variance + epsilon)
    scaled = centred * inv_std
    return (scaled * gain + shift, scaled, inv_std)


def norm_backward(incoming, scaled, inv_std, gain):
    weighted = incoming * gain
    first_mean = jnp.mean(weighted, axis=-1, keepdims=True)
    second_mean = jnp.mean(weighted * scaled, axis=-1, keepdims=True)
    return inv_std * (weighted - first_mean - scaled * second_mean)


def gelu_value(values):
    return 0.5 * values * (1.0 + lax.erf(values / math.sqrt(2.0)))


def gelu_slope(values):
    return 0.5 * (1.0 + lax.erf(values / math.sqrt(2.0))) + values * jnp.exp(
        -0.5 * values * values
    ) / math.sqrt(2.0 * math.pi)


def per_device(
    inputs,
    cotangent,
    first_gain,
    first_shift,
    token_in,
    token_in_bias,
    token_out,
    second_gain,
    second_shift,
    channel_in,
    channel_in_bias,
    channel_out,
):
    f32 = jnp.float32
    images, patches, channels = inputs.shape
    x_float = inputs.astype(f32)
    g_float = cotangent.astype(f32)
    normed_one, first_hat, first_rstd = norm_forward(x_float, first_gain, first_shift)
    normed1 = normed_one.astype(jnp.bfloat16)
    hidden1 = (
        jnp.einsum("bpc,sp->bcs", normed1, token_in, preferred_element_type=f32) + token_in_bias
    )
    act1 = gelu_value(hidden1).astype(jnp.bfloat16)
    mixed = x_float + jnp.einsum("bcs,sp->bpc", act1, token_out, preferred_element_type=f32)
    normed_two, second_hat, second_rstd = norm_forward(mixed, second_gain, second_shift)
    normed2 = normed_two.astype(jnp.bfloat16).reshape(-1, channels)
    hidden2 = jnp.dot(normed2, channel_in, preferred_element_type=f32) + channel_in_bias
    act2 = gelu_value(hidden2).astype(jnp.bfloat16)
    cot_rows = cotangent.reshape(-1, channels)
    piece = cot_rows
    chout_part = summed_rows(
        jnp.einsum("tc,tk->ck", piece, act2, preferred_element_type=f32),
        ("dev_0", "dev_1", "dev_2"),
        "dev_3",
        0,
    )
    dact2 = jnp.dot(cot_rows, channel_out, preferred_element_type=f32)
    dhidden2 = (dact2 * gelu_slope(hidden2)).astype(jnp.bfloat16)
    piece = normed2
    chin_part = summed_rows(
        jnp.einsum("tc,tk->ck", piece, dhidden2, preferred_element_type=f32),
        ("dev_0", "dev_1", "dev_2"),
        "dev_3",
        0,
    )
    dnormed2 = jnp.einsum("tk,ck->tc", dhidden2, channel_in, preferred_element_type=f32).reshape(
        images, patches, channels
    )
    dmixed = g_float + norm_backward(dnormed2, second_hat, second_rstd, second_gain)
    dmixed_round = dmixed.astype(jnp.bfloat16)
    dact1 = jnp.einsum("bpc,sp->bcs", dmixed_round, token_out, preferred_element_type=f32)
    dhidden1 = (dact1 * gelu_slope(hidden1)).astype(jnp.bfloat16)
    dnormed1 = jnp.einsum("bcs,sp->bpc", dhidden1, token_in, preferred_element_type=f32)
    grad_inputs = (dmixed + norm_backward(dnormed1, first_hat, first_rstd, first_gain)).astype(
        jnp.bfloat16
    )
    grad_in_piece = jnp.einsum("bcs,bpc->sp", dhidden1, normed1, preferred_element_type=f32)
    grad_out_piece = jnp.einsum("bcs,bpc->sp", act1, dmixed_round, preferred_element_type=f32)
    token_part = summed_on_arrival(jnp.concatenate([grad_in_piece, grad_out_piece], axis=1), DEV, 0)
    token_part, chin_part, chout_part = together((token_part, chin_part, chout_part), "grp")
    norms_part = jnp.stack(
        [
            jnp.sum(dnormed1 * first_hat, axis=(0, 1)),
            jnp.sum(dnormed1, axis=(0, 1)),
            jnp.sum(dnormed2 * second_hat, axis=(0, 1)),
            jnp.sum(dnormed2, axis=(0, 1)),
            jnp.sum(g_float, axis=(0, 1)),
        ]
    )
    tb_in = jnp.sum(dhidden1.astype(f32), axis=(0, 1))
    tb_out = jnp.sum(dmixed, axis=(0, 2))
    cb_in = jnp.sum(dhidden2.astype(f32), axis=0)
    norms_total, tb_in_total, tb_out_total, cb_in_total = together_2(
        (norms_part, tb_in, tb_out, cb_in), GRP_DEV
    )
    return (
        grad_inputs,
        token_part[:, :patches],
        token_part[:, patches:],
        chin_part,
        chout_part,
        norms_total,
        tb_in_total,
        tb_out_total,
        cb_in_total,
    )


def solution(mesh):
    split = Mesh(
        mesh.devices.reshape(mesh.shape["grp"], 4, 2, 4, 2),
        ("grp", "dev_0", "dev_1", "dev_2", "dev_3"),
    )
    in_specs = (
        P(GRP_DEV, None, None),
        P(GRP_DEV, None, None),
        P(),
        P(),
        P(),
        P(),
        P(),
        P(),
        P(),
        P(),
        P(),
        P(),
    )
    out_specs = (
        P(GRP_DEV, None, None),
        P(DEV, None),
        P(DEV, None),
        P(DEV, None),
        P(DEV, None),
        P(),
        P(),
        P(),
        P(),
    )
    return jax.shard_map(
        per_device, mesh=split, in_specs=in_specs, out_specs=out_specs, check_vma=False
    )
```

profile of v0, /device:TPU:0, one launch (start us, length us, event | category | flops | bytes accessed | tf_op | source)
XLA Modules:
  0.0 509.9 jit_solution(6757649746688285619)
XLA Ops:
  11.7 3.1 multiply_convert_fusion.1
  17.0 6.0 %fusion.50 = f32[392,4096]{1,0:T(8,128)S(1)} fusion(bf16[392,1024]{1,0:T(8,128)(2,1)S(1)} %reshape.112, bf16[1024,4096]{1,0:T(8,128)(2,1)} %param.21), kind=kOutput, calls=%fused_computation.80 | convolution fusion | flops 3288334336 | bytes 15613952 | tf_op jit(solution)/shard_map/dot_general | solution.py:115
  23.1 5.6 %fusion.12 = f32[4096,1024]{0,1:T(8,128)S(1)} fusion(bf16[392,1024]{1,0:T(8,128)(2,1)S(1)} %copy-done.11, f32[392,4096]{1,0:T(8,128)S(1)} %fusion.50, f32[4096]{0:T(1024)S(1)} %copy-done.18), kind=kOutput, calls=%fused_computation.21 | convolution fusion | flops 3297968128 | bytes 24018944 | tf_op jit(solution)/shard_map/tc,tk->ck/dot_general | solution.py:120
  28.8 6.0 %copy.55 = f32[32,2,16,4096]{3,2,0,1:T(8,128)} copy(f32[32,2,16,4096]{3,2,1,0:T(8,128)S(1)} %bitcast.73) | data formatting | bytes 33554432 | tf_op jit(solution)/shard_map/reshape;reshape | solution.py:25
  36.3 8.7 %convert_reduce_fusion = (f32[4096]{0:T(1024)S(1)}, bf16[392,4096]{1,0:T(8,128)(2,1)S(1)}) fusion(f32[392,4096]{1,0:T(8,128)} %copy-done.21, f32[4096]{0:T(1024)S(1)} %copy-done.18, bf16[392,1024]{1,0:T(8,128)(2,1)S(1)} %copy-done.11, bf16[1024,4096]{1,0:T(8,128)(2,1)} %param.23), kind=kOutput, calls=%fused_computation.8 | convolution fusion | flops 3309203456 | bytes 18857984 | tf_op jit(solution)/shard_map/dot_general | solution.py:125
  45.1 4.5 convolution_bitcast_fusion
  49.6 10.6 %copy.54 = f32[2,32,16,4096]{3,2,1,0:T(8,128)} copy(f32[2,32,16,4096]{3,2,0,1:T(8,128)S(1)} %convolution_bitcast_fusion) | data formatting | bytes 33554432 | tf_op jit(solution)/shard_map/transpose | solution.py:25
  60.3 5.0 reduce-scatter.9.cloned.1.call-done
  65.6 31.4 %reduce-scatter.5.cloned.1.call-done = f32[32,16,4096]{2,1,0:T(8,128)} async-done(((f32[64,16,4096]{2,1,0:T(8,128)}), f32[32,16,4096]{2,1,0:T(8,128)}) %reduce-scatter.5.cloned.1.call-update) | async-done | bytes 8388624 | tf_op jit(solution)/shard_map/reduce_scatter | solution.py:26
  97.0 9.1 %fusion.45 = (f32[1024]{0:T(1024)S(1)}, f32[392]{0:T(512)S(1)}, f32[392,1024]{1,0:T(8,128)}) fusion(f32[1024]{0:T(1024)S(1)} %copy-done.15, bf16[392,4096]{1,0:T(8,128)(2,1)} %copy-done.24, bf16[1024,4096]{1,0:T(8,128)(2,1)} %param.21), kind=kOutput, calls=%fused_computation.75 | convolution fusion | flops 3289537024 | bytes 13215264 | tf_op jit(solution)/shard_map/tk,ck->tc/dot_general | solution.py:134
  112.5 2.4 convert_reduce_fusion.1
  117.6 9.1 %all-to-all-start = ((f32[64,8,392]{2,1,0:T(8,128)}), f32[64,8,392]{2,1,0:T(8,128)}, u32[]{:S(2)}, u32[]{:S(2)}) async-start(f32[64,8,392]{2,1,0:T(8,128)} %bitcast.6), calls=%async_computation | async-start | bytes 2097152 | tf_op jit(solution)/shard_map/all_to_all | solution.py:32
  126.7 2.7 fusion.29
  129.7 81.2 %psum.7 = f32[9924]{0:T(1024)S(1)} all-reduce(f32[9924]{0:T(1024)S(1)} %concatenate.11), channel_id=1, replica_groups=mesh['grp'=2,'dev_0'=4,'dev_1'=2,'dev_2'=4,'dev_3'=2] {'grp','dev_0','de..., use_global_device_ids=true, to_apply=%region_22.0 | all-reduce | flops 9924 | bytes 79392 | tf_op jit(solution)/shard_map/psum | solution.py:59
  214.1 74.2 %reduce-scatter.11.cloned.1.call-done = f32[1,16,4096]{2,1,0:T(8,128)} async-done(((f32[32,16,4096]{2,1,0:T(8,128)}), f32[1,16,4096]{2,1,0:T(8,128)}) %reduce-scatter.11.cloned.1.call-update) | async-done | bytes 262160 | tf_op jit(solution)/shard_map/reduce_scatter | solution.py:27
  289.3 181.6 %reduce-scatter.7.cloned.1.call-done = f32[1,16,4096]{2,1,0:T(8,128)} async-done(((f32[32,16,4096]{2,1,0:T(8,128)}), f32[1,16,4096]{2,1,0:T(8,128)}) %reduce-scatter.7.cloned.1.call-update) | async-done | bytes 262160 | tf_op jit(solution)/shard_map/reduce_scatter | solution.py:27
  470.9 1.7 copy.63
  472.6 4.4 concatenate.10
  477.1 3.3 broadcast_in_dim.2
  480.4 4.6 all-to-all-start.1
  485.0 2.1 fusion.28
  487.0 1.7 copy.57
  489.4 6.7 %all-to-all-done.1 = f32[2,1,134208]{2,1,0:T(1,128)} async-done(((f32[2,1,134208]{2,1,0:T(1,128)}), f32[2,1,134208]{2,1,0:T(1,128)}, u32[]{:S(2)}, u32[]{:S(2)}) %all-to-all-start.1) | async-done | bytes 1073696 | tf_op jit(solution)/shard_map/all_to_all | solution.py:38
  496.1 4.8 reduce_sum.171
  (102 shorter events, 25.2 us)
Async XLA Ops:
  7.2 4.5 copy-start
  7.2 3.2 copy-start.8
  7.2 58.1 %reduce-scatter.9.cloned.1.call-start = ((), (), s32[]{:S(2)}) async-start(), calls=%async_computation.8 | async-start | bytes 25165824 | tf_op jit(solution)/shard_map/reduce_scatter | solution.py:26
  8.8 2.9 copy-start.3
  8.8 2.9 copy-start.17
  8.8 2.9 copy-start.19
  8.8 2.9 copy-start.20
  11.7 3.1 copy-start.12
  17.0 6.0 %copy-start.11 = (bf16[392,1024]{1,0:T(8,128)(2,1)S(1)}, bf16[392,1024]{1,0:T(8,128)(2,1)}, u32[]{:S(2)}) copy-start(bf16[392,1024]{1,0:T(8,128)(2,1)} %reshape.111) | copy-start | bytes 2408452
  17.0 6.0 %copy-start.18 = (f32[4096]{0:T(1024)S(1)}, f32[4096]{0:T(1024)}, u32[]{:S(2)}) copy-start(f32[4096]{0:T(1024)} %param.22) | copy-start | bytes 49156
  23.1 5.7 %copy-start.21 = (f32[392,4096]{1,0:T(8,128)}, f32[392,4096]{1,0:T(8,128)S(1)}, u32[]{:S(2)}) copy-start(f32[392,4096]{1,0:T(8,128)S(1)} %fusion.50) | copy-start | bytes 19267588
  34.8 62.2 %reduce-scatter.5.cloned.1.call-start = ((), (), s32[]{:S(2)}) async-start(), calls=%async_computation.6 | async-start | bytes 25165824 | tf_op jit(solution)/shard_map/reduce_scatter | solution.py:26
  36.3 8.7 %copy-start.10 = (bf16[1024,392]{1,0:T(8,128)(2,1)S(1)}, bf16[1024,392]{1,0:T(8,128)(2,1)}, u32[]{:S(2)}) copy-start(bf16[1024,392]{1,0:T(8,128)(2,1)} %copy.53) | copy-start | bytes 2408452
  45.0 4.5 copy-start.24
  60.2 228.1 %reduce-scatter.11.cloned.1.call-start = ((), (), s32[]{:S(2)}) async-start(), calls=%async_computation.9 | async-start | bytes 8650752 | tf_op jit(solution)/shard_map/reduce_scatter | solution.py:27
  65.3 405.6 %reduce-scatter.7.cloned.1.call-start = ((), (), s32[]{:S(2)}) async-start(), calls=%async_computation.7 | async-start | bytes 8650752 | tf_op jit(solution)/shard_map/reduce_scatter | solution.py:27
  108.9 3.5 copy-start.22
  109.8 5.1 copy-start.1
  117.6 95.1 %all-to-all-start = ((f32[64,8,392]{2,1,0:T(8,128)}), f32[64,8,392]{2,1,0:T(8,128)}, u32[]{:S(2)}, u32[]{:S(2)}) async-start(f32[64,8,392]{2,1,0:T(8,128)} %bitcast.6), calls=%async_computation | async-start | bytes 2097152 | tf_op jit(solution)/shard_map/all_to_all | solution.py:32
  129.4 343.2 %copy-start.7 = (f32[2,1024,196]{1,2,0:T(8,128)}, f32[2,1024,196]{1,2,0:T(8,128)S(1)}, u32[]{:S(2)}) copy-start(f32[2,1024,196]{1,2,0:T(8,128)S(1)} %get-tuple-element.73) | copy-start | bytes 4816900
  210.9 269.5 %copy-start.14 = (f32[9924]{0:T(1024)}, f32[9924]{0:T(1024)S(1)}, u32[]{:S(2)}) copy-start(f32[9924]{0:T(1024)S(1)} %psum.7) | copy-start | bytes 119092
  477.0 7.9 %copy-start.2 = (f32[2,196,1024]{2,1,0:T(8,128)S(1)}, f32[2,196,1024]{2,1,0:T(8,128)}, u32[]{:S(2)}) copy-start(f32[2,196,1024]{2,1,0:T(8,128)} %copy-done.1) | copy-start | bytes 4816900
  480.4 15.7 %all-to-all-start.1 = ((f32[2,1,134208]{2,1,0:T(1,128)}), f32[2,1,134208]{2,1,0:T(1,128)}, u32[]{:S(2)}, u32[]{:S(2)}) async-start(f32[2,1,134208]{2,1,0:T(1,128)} %broadcast_in_dim.2), calls=%async_computation.5 | async-start | bytes 2148352 | tf_op jit(solution)/shard_map/all_to_all | solution.py:38
  485.0 3.8 slice-start
  (8 other events, 14.0 us)
Sparse Core Ops, SparseCore 0:
  34.9 30.3 reduce-scatter.8
  67.7 29.2 reduce-scatter.4
  99.4 188.9 reduce-scatter.10
  290.6 180.2 reduce-scatter.6
where the time goes:
time: 511 us; the launch traced here: 510 us
  waiting for transfers between devices  299 us (59%)
  blocking collectives  81.2 us (16%)
  matrix products  44.3 us (9%)
  local copies, waits for them, and re-layouts  43.4 us (8%)
  starting transfers between devices  14.2 us (3%)
  between operations  14.2 us (3%)
  other arithmetic  13.7 us (3%)
    reduce_scatter x2, waiting for transfers between devices, summed_rows(): return lax.psum_scatter(blocks, chips, scatter_dimension=0, tiled=True)[0]  256 us
    psum x1, blocking collectives, together_2(): running = lax.psum(jnp.concatenate([a.ravel() for a in arrays]), axis)  81.2 us
    reduce_scatter x2, waiting for transfers between devices, summed_rows(): blocks = lax.psum_scatter(blocks, core, scatter_dimension=0, tiled=True)  36.4 us
    transpose x1, local copies, waits for them, and re-layouts, summed_rows(): blocks = blocks.reshape(*sizes, *inside).swapaxes(0, 1).reshape(-1, *inside)  10.6 us
  transfers between devices with their start and end apart: 6, of which 5 were waited for; matrix products, arithmetic and copies ran while one was open for 11% of the time, Pallas kernels for 0%

commit v1 on v0

--- a/solution.py
+++ b/solution.py
@@ -3,28 +3,374 @@
 import jax
 import jax.numpy as jnp
 from jax import lax
+from jax.experimental import pallas as pl
+from jax.experimental.pallas import tpu as pltpu
 from jax.sharding import Mesh
 from jax.sharding import PartitionSpec as P
 
 DEV = ("dev_0", "dev_1", "dev_2", "dev_3")
 GRP_DEV = ("grp", "dev_0", "dev_1", "dev_2", "dev_3")
-
+MESH = pl.DeviceIdType.MESH
 
 epsilon = 1e-06
+
+CHUNKS = 8
+WIDTH = 512
+ROWS = 400
+COLOURS = (("x", "z", "y", 384), ("y", "z", "x", 384), ("z", "x", "y", 256))
+FIRST = (0, 384, 768)
+LAG = (0, 2, 5, 8, 11, 14, 17, 20)
+SLOTS = CHUNKS + (LAG[-1] + 1) // 2
+
+
+def remainder(a, b):
+    return lax.rem(a, jnp.int32(b))
+
+
+def where_on(fixed, half=None):
+    index = [slice(None)] * 4
+    for axis, at in fixed.items():
+        if axis == "x":
+            index[0] = at
+        elif axis == "y":
+            index[2] = at
+        else:
+            index[1] = remainder(at, 2)
+            index[3] = lax.div(at, jnp.int32(2))
+    if half is not None:
+        axis, part = half
+        if axis == "z_lo":
+            index[1] = part
+        else:
+            index[0 if axis == "x" else 2] = pl.ds(2 * part, 2)
+    return tuple(index)
+
+
+HALVES = (("z_lo", "y"), ("z_lo", "x"), ("x", "y"))
+HALF_SHAPES = (((4, 2), (2,)), ((4, 2), (2,)), ((2, 4), (2,)))
+BLOCK_SHAPES = (((2, 4, 2), (4,)), ((4, 2, 2), (4,)), ((4, 4), (4,)))
+
+
+def scratch_of():
+    f32, bf16, dma = jnp.float32, jnp.bfloat16, pltpu.SemaphoreType.DMA
+    shapes = {}
+    for c, (_, _, _, width) in enumerate(COLOURS):
+        shapes[f"own{c}"] = pltpu.VMEM((2, 4, 2, 4, 2, 2, 8, width), f32)
+        shapes[f"sum{c}"] = pltpu.VMEM((CHUNKS, 4, 2, 4, 2, 8, width), f32)
+        for p in range(2):
+            shapes[f"half{c}{p}"] = pltpu.VMEM((CHUNKS, 2, *HALF_SHAPES[c][p], 8, width), f32)
+            shapes[f"block{c}{p}"] = pltpu.VMEM((CHUNKS, 2, *BLOCK_SHAPES[c][p], 8, width), f32)
+        shapes[f"last{c}"] = pltpu.VMEM((CHUNKS, 3, 8, width), f32)
+    shapes["done"] = pltpu.VMEM((2, CHUNKS, 8, 2 * WIDTH), f32)
+    shapes["w_in"] = pltpu.VMEM((2, 1024, WIDTH), bf16)
+    shapes["w_out"] = pltpu.VMEM((2, 1024, WIDTH), bf16)
+    shapes["act"] = pltpu.VMEM((512, WIDTH), bf16)
+    shapes["dhid"] = pltpu.VMEM((512, WIDTH), bf16)
+    shapes["hid"] = pltpu.VMEM((ROWS, WIDTH), f32)
+    shapes["dact"] = pltpu.VMEM((ROWS, WIDTH), f32)
+    shapes["w_sem"] = dma((2, 2))
+    shapes["pair_send"] = dma((3,))
+    shapes["pair_recv"] = dma((CHUNKS, 3))
+    for p in range(2):
+        shapes[f"half_send{p}"] = dma((3, 2))
+        shapes[f"half_recv{p}"] = dma((CHUNKS, 3, 2))
+        shapes[f"block_send{p}"] = dma((3, 2))
+        shapes[f"block_recv{p}"] = dma((CHUNKS, 3, 2))
+    shapes["last_send"] = dma((3, 3))
+    shapes["last_recv"] = dma((CHUNKS, 3, 3))
+    shapes["both_send"] = dma((1,))
+    shapes["both_recv"] = dma((CHUNKS,))
+    return shapes
+
+
+def channel_kernel(names, n2, n2t, cot, cott, win, wout, bias, dn2, grads, cb, *scratch):
+    r = dict(zip(names, scratch))
+    f32, bf16 = jnp.float32, jnp.bfloat16
+    x, y, core = lax.axis_index("dev_0"), lax.axis_index("dev_2"), lax.axis_index("dev_3")
+    high = lax.axis_index("grp")
+    me = {"x": x, "y": y, "z": 2 * high + lax.axis_index("dev_1")}
+
+    def device(core=core, **moved):
+        at = {**me, **moved}
+        return (lax.div(at["z"], jnp.int32(2)), at["x"], remainder(at["z"], 2), at["y"], core)
+
+    def along(axis, by):
+        return remainder(me[axis] + by, 4)
+
+    partners = [device(core=1 - core)]
+    for axis in ("x", "y", "z"):
+        partners += [device(**{axis: along(axis, by)}) for by in (1, 2, 3)]
+    barrier = pltpu.get_barrier_semaphore()
+    for partner in partners:
+        pl.semaphore_signal(barrier, inc=1, device_id=partner, device_id_type=MESH)
+    pl.semaphore_wait(barrier, len(partners))
+
+    def remote(source, target, send, recv, to):
+        return pltpu.make_async_remote_copy(
+            src_ref=source, dst_ref=target, send_sem=send, recv_sem=recv, device_id=to, device_id_type=MESH
+        )
+
+    def fixed_before(c, p):
+        return {axis: me[axis] for axis in COLOURS[c][:p]}
+
+    def pair_copies(j):
+        slot = remainder(j, 2)
+        every = slice(None)
+        return [
+            remote(
+                r[f"own{c}"].at[slot, every, every, every, 1 - core],
+                r[f"sum{c}"].at[j],
+                r["pair_send"].at[c],
+                r["pair_recv"].at[j, c],
+                device(core=1 - core),
+            )
+            for c in range(3)
+        ]
+
+    def half_copies(j, p):
+        copies = []
+        for c in range(3):
+            axis = COLOURS[c][p]
+            for d, by in enumerate((1, 3)):
+                spot = where_on({**fixed_before(c, p), axis: along(axis, 2)}, (HALVES[c][p], d))
+                copies.append(
+                    remote(
+                        r[f"sum{c}"].at[(j, *spot)],
+                        r[f"half{c}{p}"].at[j, d],
+                        r[f"half_send{p}"].at[c, d],
+                        r[f"half_recv{p}"].at[j, c, d],
+                        device(**{axis: along(axis, by)}),
+                    )
+                )
+        return copies
+
+    def block_copies(j, p):
+        copies = []
+        for c in range(3):
+            axis = COLOURS[c][p]
+            for d, by in enumerate((1, 3)):
+                spot = where_on({**fixed_before(c, p), axis: along(axis, by)})
+                copies.append(
+                    remote(
+                        r[f"sum{c}"].at[(j, *spot)],
+                        r[f"block{c}{p}"].at[j, d],
+                        r[f"block_send{p}"].at[c, d],
+                        r[f"block_recv{p}"].at[j, c, d],
+                        device(**{axis: along(axis, by)}),
+                    )
+                )
+        return copies
+
+    def last_copies(j):
+        copies = []
+        for c in range(3):
+            axis = COLOURS[c][2]
+            for d, by in enumerate((1, 2, 3)):
+                spot = where_on({**fixed_before(c, 2), axis: along(axis, by)})
+                copies.append(
+                    remote(
+                        r[f"sum{c}"].at[(j, *spot)],
+                        r[f"last{c}"].at[j, d],
+                        r["last_send"].at[c, d],
+                        r["last_recv"].at[j, c, d],
+                        device(**{axis: along(axis, by)}),
+                    )
+                )
+        return copies
+
+    def both_copy(j):
+        return remote(
+            r["done"].at[high, j],
+            r["done"].at[high, j],
+            r["both_send"].at[0],
+            r["both_recv"].at[j],
+            device(z=along("z", 2)),
+        )
+
+    def start(copies):
+        for copy in copies:
+            copy.start()
+
+    def wait(copies):
+        for copy in copies:
+            copy.wait()
+
+    def stage(s, j):
+        if s == 1:
+            wait(pair_copies(j))
+            slot = remainder(j, 2)
+            for c in range(3):
+                for b in range(4):
+                    r[f"sum{c}"][j, b] += r[f"own{c}"][slot, b, :, :, core]
+            start(half_copies(j, 0))
+        elif s in (2, 4):
+            p = s // 2 - 1
+            wait(half_copies(j, p))
+            for c in range(3):
+                axis = COLOURS[c][p]
+                for d, by in enumerate((1, 3)):
+                    spot = where_on({**fixed_before(c, p), axis: along(axis, by)}, (HALVES[c][p], d))
+                    r[f"sum{c}"][(j, *spot)] += r[f"half{c}{p}"][j, d]
+            start(block_copies(j, p))
+        elif s in (3, 5):
+            p = s // 2 - 1
+            wait(block_copies(j, p))
+            for c in range(3):
+                spot = where_on(fixed_before(c, p + 1))
+                r[f"sum{c}"][(j, *spot)] += r[f"block{c}{p}"][j, 0] + r[f"block{c}{p}"][j, 1]
+            start(half_copies(j, 1) if p == 0 else last_copies(j))
+        elif s == 6:
+            wait(last_copies(j))
+            for c in range(3):
+                width = COLOURS[c][3]
+                spot = where_on(me)
+                got = r[f"last{c}"]
+                r["done"][high, j, :, FIRST[c] : FIRST[c] + width] = (
+                    r[f"sum{c}"][(j, *spot)] + got[j, 0] + (got[j, 1] + got[j, 2])
+                )
+            start([both_copy(j)])
+        else:
+            wait([both_copy(j)])
+
+    def tick(t, parity):
+        for s in range(7, 0, -1):
+            if (LAG[s] - parity) % 2 == 0:
+                j = t - (LAG[s] - parity) // 2
+
+                @pl.when((j >= 0) & (j < CHUNKS))
+                def _():
+                    stage(s, j)
+
+    def weights(j):
+        slot = remainder(j, 2)
+        columns = pl.ds(pl.multiple_of(j * WIDTH, WIDTH), WIDTH)
+        return [
+            pltpu.make_async_copy(win.at[:, columns], r["w_in"].at[slot], r["w_sem"].at[slot, 0]),
+            pltpu.make_async_copy(wout.at[:, columns], r["w_out"].at[slot], r["w_sem"].at[slot, 1]),
+        ]
+
+    act, dhid, hid, dact = r["act"], r["dhid"], r["hid"], r["dact"]
+
+    def forward(j):
+        slot = remainder(j, 2)
+        wait(weights(j))
+
+        @pl.when(j + 1 < CHUNKS)
+        def _():
+            start(weights(j + 1))
+
+        columns = pl.ds(pl.multiple_of(j * WIDTH, WIDTH), WIDTH)
+        for b in range(WIDTH // 256):
+            part = slice(256 * b, 256 * (b + 1))
+            hid[:, part] = jnp.dot(n2[...], r["w_in"][slot, :, part], preferred_element_type=f32)
+            dact[:, part] = jnp.dot(cot[...], r["w_out"][slot, :, part], preferred_element_type=f32)
+        shift = bias[:, columns]
+
+        def rows(i, total):
+            at = pl.ds(pl.multiple_of(i * 80, 80), 80)
+            v = hid[at, :] + shift
+            twice = 1.0 + lax.erf(v * (1.0 / math.sqrt(2.0)))
+            act[at, :] = (0.5 * v * twice).astype(bf16)
+            slope = 0.5 * twice + v * jnp.exp(-0.5 * v * v) * (1.0 / math.sqrt(2.0 * math.pi))
+            d = (dact[at, :] * slope).astype(bf16)
+            dhid[at, :] = d
+            return total + jnp.sum(d.astype(f32).reshape(10, 8, WIDTH), axis=0)
+
+        total = lax.fori_loop(0, ROWS // 80, rows, jnp.zeros((8, WIDTH), f32))
+        cb[:, columns] = jnp.sum(total, axis=0, keepdims=True)
+
+    def gradients(j):
+        slot = remainder(j, 2)
+
+        def rows(i, _):
+            at = pl.ds(pl.multiple_of(i * 256, 256), 256)
+            out = jnp.dot(cott[at, :], act[...], preferred_element_type=f32).reshape(2, 4, 2, 2, 8, WIDTH)
+            r["own0"][slot, i] = out[..., :384]
+            r["own1"][slot, i, :, :, :, :, :, :128] = out[..., 384:]
+            inn = jnp.dot(n2t[at, :], dhid[...], preferred_element_type=f32).reshape(2, 4, 2, 2, 8, WIDTH)
+            r["own1"][slot, i, :, :, :, :, :, 128:] = inn[..., :256]
+            r["own2"][slot, i] = inn[..., 256:]
+            return 0
+
+        lax.fori_loop(0, 4, rows, 0)
+        start(pair_copies(j))
+        for b in range(4):
+            part = slice(256 * b, 256 * (b + 1))
+            dn2[:, part] += lax.dot_general(
+                dhid[:ROWS, :],
+                r["w_in"][slot, part, :],
+                (((1,), (1,)), ((), ())),
+                preferred_element_type=f32,
+            )
+
+    start(weights(jnp.int32(0)))
+    act[ROWS:, :] = jnp.zeros((512 - ROWS, WIDTH), bf16)
+    dhid[ROWS:, :] = jnp.zeros((512 - ROWS, WIDTH), bf16)
+    dn2[...] = jnp.zeros_like(dn2)
+
+    def slot_of(t, _):
+        @pl.when(t < CHUNKS)
+        def _():
+            forward(t)
+
+        tick(t, 0)
+
+        @pl.when(t < CHUNKS)
+        def _():
+            gradients(t)
+
+        tick(t, 1)
+        return 0
+
+    lax.fori_loop(0, SLOTS, slot_of, 0)
+    for h in range(2):
+        for j in range(CHUNKS):
+            for g in range(2):
+                grads[g, 8 * h : 8 * (h + 1), WIDTH * j : WIDTH * (j + 1)] = r["done"][
+                    h, j, :, WIDTH * g : WIDTH * (g + 1)
+                ]
+
+
+def channel_stage(normed2, cot_rows, channel_in, channel_out, channel_in_bias):
+    f32 = jnp.float32
+    tokens, channels = normed2.shape
+    hidden = channel_in.shape[1]
+    down = lambda a: jnp.pad(a, ((0, ROWS - tokens), (0, 0)))
+    across = lambda a: jnp.pad(a.T, ((0, 0), (0, 512 - tokens)))
+    shapes = scratch_of()
+    vmem, anywhere = pl.BlockSpec(memory_space=pltpu.VMEM), pl.BlockSpec(memory_space=pl.ANY)
+    names = tuple(shapes)
+
+    def kernel(*refs):
+        channel_kernel(names, *refs)
+
+    dn2, grads, cb = pl.pallas_call(
+        kernel,
+        out_shape=(
+            jax.ShapeDtypeStruct((ROWS, channels), f32),
+            jax.ShapeDtypeStruct((2, 16, hidden), f32),
+            jax.ShapeDtypeStruct((1, hidden), f32),
+        ),
+        in_specs=[vmem, vmem, vmem, vmem, anywhere, anywhere, vmem],
+        out_specs=(vmem, vmem, vmem),
+        scratch_shapes=list(shapes.values()),
+        compiler_params=pltpu.CompilerParams(collective_id=0, has_side_effects=True, vmem_limit_bytes=66_000_000),
+        name="channel_stage",
+    )(
+        down(normed2),
+        across(normed2),
+        down(cot_rows),
+        across(cot_rows),
+        channel_in,
+        channel_out,
+        channel_in_bias.reshape(1, -1),
+    )
+    return dn2[:tokens], grads[0], grads[1], cb[0]
 
 
 def cut_along(shard, dim, count):
     before, after = (shard.shape[:dim], shard.shape[dim + 1 :])
     return jnp.moveaxis(shard.reshape(*before, count, -1, *after), dim, 0)
-
-
-def summed_rows(shard, chips, core, dim):
-    sizes = (lax.axis_size(chips), lax.axis_size(core))
-    blocks = cut_along(shard, dim, sizes[0] * sizes[1])
-    inside = blocks.shape[1:]
-    blocks = blocks.reshape(*sizes, *inside).swapaxes(0, 1).reshape(-1, *inside)
-    blocks = lax.psum_scatter(blocks, core, scatter_dimension=0, tiled=True)
-    return lax.psum_scatter(blocks, chips, scatter_dimension=0, tiled=True)[0]
 
 
 def summed_on_arrival(shard, axis, dim):
@@ -112,28 +458,11 @@
     mixed = x_float + jnp.einsum("bcs,sp->bpc", act1, token_out, preferred_element_type=f32)
     normed_two, second_hat, second_rstd = norm_forward(mixed, second_gain, second_shift)
     normed2 = normed_two.astype(jnp.bfloat16).reshape(-1, channels)
-    hidden2 = jnp.dot(normed2, channel_in, preferred_element_type=f32) + channel_in_bias
-    act2 = gelu_value(hidden2).astype(jnp.bfloat16)
     cot_rows = cotangent.reshape(-1, channels)
-    piece = cot_rows
-    chout_part = summed_rows(
-        jnp.einsum("tc,tk->ck", piece, act2, preferred_element_type=f32),
-        ("dev_0", "dev_1", "dev_2"),
-        "dev_3",
-        0,
-    )
-    dact2 = jnp.dot(cot_rows, channel_out, preferred_element_type=f32)
-    dhidden2 = (dact2 * gelu_slope(hidden2)).astype(jnp.bfloat16)
-    piece = normed2
-    chin_part = summed_rows(
-        jnp.einsum("tc,tk->ck", piece, dhidden2, preferred_element_type=f32),
-        ("dev_0", "dev_1", "dev_2"),
-        "dev_3",
-        0,
-    )
-    dnormed2 = jnp.einsum("tk,ck->tc", dhidden2, channel_in, preferred_element_type=f32).reshape(
-        images, patches, channels
-    )
+    dnormed2, chout_part, chin_part, cb_in = channel_stage(
+        normed2, cot_rows, channel_in, channel_out, channel_in_bias
+    )
+    dnormed2 = dnormed2.reshape(images, patches, channels)
     dmixed = g_float + norm_backward(dnormed2, second_hat, second_rstd, second_gain)
     dmixed_round = dmixed.astype(jnp.bfloat16)
     dact1 = jnp.einsum("bpc,sp->bcs", dmixed_round, token_out, preferred_element_type=f32)
@@ -145,7 +474,7 @@
     grad_in_piece = jnp.einsum("bcs,bpc->sp", dhidden1, normed1, preferred_element_type=f32)
     grad_out_piece = jnp.einsum("bcs,bpc->sp", act1, dmixed_round, preferred_element_type=f32)
     token_part = summed_on_arrival(jnp.concatenate([grad_in_piece, grad_out_piece], axis=1), DEV, 0)
-    token_part, chin_part, chout_part = together((token_part, chin_part, chout_part), "grp")
+    (token_part,) = together((token_part,), "grp")
     norms_part = jnp.stack(
         [
             jnp.sum(dnormed1 * first_hat, axis=(0, 1)),
@@ -157,7 +486,6 @@
     )
     tb_in = jnp.sum(dhidden1.astype(f32), axis=(0, 1))
     tb_out = jnp.sum(dmixed, axis=(0, 2))
-    cb_in = jnp.sum(dhidden2.astype(f32), axis=0)
     norms_total, tb_in_total, tb_out_total, cb_in_total = together_2(
         (norms_part, tb_in, tb_out, cb_in), GRP_DEV
     )

time: 511 us -> 236 us (0.46)
  waiting for transfers between devices: 299 us -> 7.68 us
  Pallas kernels: 0 us -> 104 us
  matrix products: 44.3 us -> 11.3 us
  local copies, waits for them, and re-layouts: 43.4 us -> 23.1 us
  blocking collectives: 81.2 us -> 64.6 us
  between operations: 14.2 us -> 0.92 us
    reduce_scatter x4 -> x0, waiting for transfers between devices: 292 us -> none  [the longest x2 256 us: summed_rows(): return lax.psum_scatter(blocks, chips, scatter_dimension=0, tiled=True)[0]]
    pallas_call x0 -> x1, Pallas kernels: none -> 104 us  [channel_stage(): pl.pallas_call(kernel, out_shape=(jax.ShapeDtypeStruct((ROWS, channels),...]
    dot_general x5 -> x0, matrix products: 33.9 us -> none  [the longest x1 9.06 us: per_device(): jnp.einsum('tk,ck->tc', dhidden2, channel_in, preferred_element_type=f32)]
    psum x1, blocking collectives: 81.2 us -> 64.6 us  [together_2(): running = lax.psum(jnp.concatenate([a.ravel() for a in arrays]), axis)]
    transpose x1 -> x0, local copies, waits for them, and re-layouts: 10.6 us -> none  [summed_rows(): blocks = blocks.reshape(*sizes, *inside).swapaxes(0, 1).reshape(-1, *inside)]
    all_to_all x1, waiting for transfers between devices: 0.01 us -> 7.68 us  [summed_on_arrival(): lax.all_to_all(cut_along(shard, dim, count), axis, 0, 0, tiled=True)]
    all_to_all x1, waiting for transfers between devices: 6.73 us -> 0.01 us  [copy_for_each(): return lax.all_to_all(copies, axis, split_axis=0, concat_axis=0, tiled=True)]
    another operation x1 -> x0, local copies, waits for them, and re-layouts: 6.03 us -> none  [summed_rows(): blocks = blocks.reshape(*sizes, *inside).swapaxes(0, 1).reshape(-1, *inside)]
  transfers between devices with their start and end apart: 6 -> 2, of which waited for: 5 -> 1; matrix products, arithmetic and copies ran while one was open for 11% -> 6% of each run, Pallas kernels for 0% -> 0%
where the time goes in v1:
time: 236 us; the launch traced here: 235 us
  Pallas kernels  104 us (44%)
  blocking collectives  64.6 us (27%)
  local copies, waits for them, and re-layouts  23.1 us (10%)
  other arithmetic  13.3 us (6%)
  matrix products  11.3 us (5%)
  starting transfers between devices  9.63 us (4%)
  waiting for transfers between devices  7.68 us (3%)
    pallas_call x1, Pallas kernels, channel_stage(): pl.pallas_call(kernel, out_shape=(jax.ShapeDtypeStruct((ROWS, channels),...  104 us
    psum x1, blocking collectives, together_2(): running = lax.psum(jnp.concatenate([a.ravel() for a in arrays]), axis)  64.6 us
    unnamed x46, local copies, waits for them, and re-layouts  7.74 us
    all_to_all x1, waiting for transfers between devices, summed_on_arrival(): lax.all_to_all(cut_along(shard, dim, count), axis, 0, 0, tiled=True)  7.68 us
    all_to_all x1, starting transfers between devices, summed_on_arrival(): lax.all_to_all(cut_along(shard, dim, count), axis, 0, 0, tiled=True)  6.38 us
  transfers between devices with their start and end apart: 2, of which 1 were waited for; matrix products, arithmetic and copies ran while one was open for 6% of the time, Pallas kernels for 0%

profile of v1, /device:TPU:0, one launch (start us, length us, event | category | flops | bytes accessed | tf_op | source)
XLA Modules:
  0.0 234.5 jit_solution(8802270979026340131)
XLA Ops:
  0.7 1.5 convert_reduce_fusion.1
  2.2 1.5 fusion.20
  5.7 3.0 %multiply_convert_fusion = (bf16[2,1024,512]{2,1,0:T(8,128)(2,1)S(1)}, f32[2,1024,512]{2,1,0:T(8,128)}) fusion(f32[512]{0:T(512)S(1)} %copy-done.19, bf16[512,196]{0,1:T(8,128)(2,1)S(1)} %copy-done, f32[1024]{0:T(1024)S(1)} %copy-done.18, f32[1024]{0:T(1024)S(1)} %copy-done.17, f32[2,196]{1,0:T(2,128)S(1)} %add_rsqrt_fusion.1, ...), kind=kOutput, calls=%fused_computation.8 | convolution fusion | flops 419741696 | bytes 7308352 | tf_op jit(solution)/shard_map/bpc,sp->bcs/dot_general | solution.py:455
  11.7 1.0 pad.14.refs_0_
  12.7 1.3 copy.44
  14.0 1.1 pad.17.refs_3_
  15.6 1.1 pad.15.refs_1_
  16.8 104.0 %channel_stage.1 = (f32[400,1024]{1,0:T(8,128)}, f32[2,16,4096]{2,1,0:T(8,128)}, f32[1,4096]{1,0:T(1,128)}) custom-call(bf16[400,1024]{1,0:T(8,128)(2,1)} %pad.14.refs_0_, bf16[1024,512]{1,0:T(8,128)(2,1)} %pad.15.refs_1_, bf16[400,1024]{1,0:T(8,128)(2,1)} %pad.16.refs_2_, bf16[1024,512]{1,0:T(8,128)(2,1)} %pad.17.refs_3_, bf16[1024,4096]{1,0:T(8,128)(2,1)} %refs_4_.1, ...), custom_call_target="tpu_custom_call" | custom-call | tf_op jit(solution)/shard_map/channel_stage/pallas_call | solution.py:347
  120.8 2.9 %slice_reduce_fusion = (f32[1024]{0:T(1024)S(1)}, f32[392]{0:T(512)S(1)}, f32[392,1024]{1,0:T(8,128)}) fusion(f32[400,1024]{1,0:T(8,128)} %get-tuple-element.12, f32[1024]{0:T(1024)S(1)} %copy-done.14), kind=kLoop, calls=%fused_computation.61 | loop fusion | flops 1202808 | bytes 3221024 | tf_op jit(solution)/shard_map/reduce_sum | solution.py:483
  123.8 1.7 reshape.104
  128.9 1.2 copy-done.20
  130.1 2.4 %convert_reduce_fusion = (f32[512]{0:T(512)S(1)}, bf16[2,1024,512]{2,1,0:T(8,128)(2,1)S(1)}) fusion(f32[2,1024,512]{2,1,0:T(8,128)S(1)} %copy-done.20, f32[512]{0:T(512)S(1)} %copy-done.19, bf16[512,196]{0,1:T(8,128)(2,1)S(1)} %copy-done.13, f32[2,196,1024]{2,1,0:T(8,128)S(1)} %get-tuple-element.59), kind=kOutput, calls=%fused_computation.7 | convolution fusion | flops 425074176 | bytes 8101888 | tf_op jit(solution)/shard_map/bpc,sp->bcs/dot_general | solution.py:468
  132.5 1.3 copy-done.21
  134.6 1.4 copy.47
  136.0 6.4 %all-to-all-start = ((f32[64,8,392]{2,1,0:T(8,128)}), f32[64,8,392]{2,1,0:T(8,128)}, u32[]{:S(2)}, u32[]{:S(2)}) async-start(f32[64,8,392]{2,1,0:T(8,128)} %bitcast.9), calls=%async_computation | async-start | bytes 2097152 | tf_op jit(solution)/shard_map/all_to_all | solution.py:378
  142.3 3.7 %fusion.19 = (f32[1024]{0:T(1024)S(1)}, f32[2,196]{1,0:T(2,128)S(1)}, f32[2,196]{1,0:T(2,128)S(1)}, f32[2,1024,196]{1,2,0:T(8,128)}) fusion(f32[2,196]{1,0:T(2,128)S(1)} %add_rsqrt_fusion.1, f32[2,196]{1,0:T(2,128)S(1)} %broadcast_multiply_fusion.5, bf16[2,196,1024]{2,0,1:T(2,128)(2,1)S(1)} %copy-done.6, f32[1024]{0:T(1024)S(1)} %copy-done.17, ...), kind=kOutput, calls=%fused_computation.28 | convolution fusion | flops 414652672 | bytes 4720768 | tf_op jit(solution)/shard_map/bcs,sp->bpc/dot_general | solution.py:470
  146.1 1.7 reduce_sum.164
  148.0 2.1 fusion.18
  150.2 1.9 slice_bitcast_fusion
  152.0 7.7 %all-to-all-done = f32[64,8,392]{2,1,0:T(8,128)} async-done(((f32[64,8,392]{2,1,0:T(8,128)}), f32[64,8,392]{2,1,0:T(8,128)}, u32[]{:S(2)}, u32[]{:S(2)}) %all-to-all-start) | async-done | bytes 802848 | tf_op jit(solution)/shard_map/all_to_all | solution.py:378
  159.7 1.3 reduce_sum.161
  161.7 3.2 %all-to-all-start.1 = ((f32[2,1,3136]{2,1,0:T(1,128)}), f32[2,1,3136]{2,1,0:T(1,128)S(1)}, u32[]{:S(2)}, u32[]{:S(2)}) async-start(f32[2,1,3136]{2,1,0:T(1,128)} %broadcast_in_dim.5), calls=%async_computation.1 | async-start | bytes 51200 | tf_op jit(solution)/shard_map/all_to_all | solution.py:384
  165.0 64.6 %psum.7 = f32[9924]{0:T(1024)S(1)} all-reduce(f32[9924]{0:T(1024)S(1)} %concatenate.7), channel_id=1, replica_groups=mesh['grp'=2,'dev_0'=4,'dev_1'=2,'dev_2'=4,'dev_3'=2] {'grp','dev_0','de..., use_global_device_ids=true, to_apply=%region_17.18 | all-reduce | flops 9924 | bytes 79392 | tf_op jit(solution)/shard_map/psum | solution.py:405
  231.4 1.7 copy.49
  (77 shorter events, 13.9 us)
Async XLA Ops:
  0.6 5.0 %copy-start = (bf16[512,196]{0,1:T(8,128)(2,1)S(1)}, bf16[512,196]{0,1:T(8,128)(2,1)}, u32[]{:S(2)}) copy-start(bf16[512,196]{0,1:T(8,128)(2,1)} %param.16) | copy-start | bytes 602116
  0.7 3.1 %copy-start.10 = (bf16[2,196,1024]{2,0,1:T(2,128)(2,1)S(1)}, bf16[2,196,1024]{2,0,1:T(2,128)(2,1)}, u32[]{:S(2)}) copy-start(bf16[2,196,1024]{2,0,1:T(2,128)(2,1)} %param.13) | copy-start | bytes 2408452
  4.1 1.5 copy-start.5
  4.1 1.5 copy-start.17
  4.1 1.5 copy-start.18
  4.2 1.5 copy-start.19
  5.7 3.0 %copy-start.12 = (bf16[512,196]{0,1:T(8,128)(2,1)S(1)}, bf16[512,196]{0,1:T(8,128)(2,1)}, u32[]{:S(2)}) copy-start(bf16[512,196]{0,1:T(8,128)(2,1)} %param.18) | copy-start | bytes 602116
  8.7 1.3 copy-start.7
  10.0 1.2 copy-start.1
  10.0 1.2 copy-start.14
  10.0 1.2 copy-start.16
  14.0 1.6 copy-start.9
  123.7 1.9 copy-start.2
  125.6 1.1 copy-start.11
  126.7 1.6 copy-start.8
  126.7 3.4 %copy-start.20 = (f32[2,1024,512]{2,1,0:T(8,128)S(1)}, f32[2,1024,512]{2,1,0:T(8,128)}, u32[]{:S(2)}) copy-start(f32[2,1024,512]{2,1,0:T(8,128)} %get-tuple-element.67) | copy-start | bytes 12582916
  127.7 1.2 copy-start.3
  128.3 1.8 copy-start.13
  130.1 3.7 %copy-start.6 = (bf16[2,196,1024]{2,0,1:T(2,128)(2,1)S(1)}, bf16[2,196,1024]{2,0,1:T(2,128)(2,1)}, u32[]{:S(2)}) copy-start(bf16[2,196,1024]{2,0,1:T(2,128)(2,1)} %param.12) | copy-start | bytes 2408452
  132.5 1.4 copy-start.21
  136.0 23.7 %all-to-all-start = ((f32[64,8,392]{2,1,0:T(8,128)}), f32[64,8,392]{2,1,0:T(8,128)}, u32[]{:S(2)}, u32[]{:S(2)}) async-start(f32[64,8,392]{2,1,0:T(8,128)} %bitcast.9), calls=%async_computation | async-start | bytes 2097152 | tf_op jit(solution)/shard_map/all_to_all | solution.py:378
  146.1 1.9 copy-start.4
  148.0 2.1 copy-start.15
  161.7 72.0 %all-to-all-start.1 = ((f32[2,1,3136]{2,1,0:T(1,128)}), f32[2,1,3136]{2,1,0:T(1,128)S(1)}, u32[]{:S(2)}, u32[]{:S(2)}) async-start(f32[2,1,3136]{2,1,0:T(1,128)} %broadcast_in_dim.5), calls=%async_computation.1 | async-start | bytes 51200 | tf_op jit(solution)/shard_map/all_to_all | solution.py:384

commit v2 on v1

v2 whole, which is shorter than its diff:
```python
import math

import jax
import jax.numpy as jnp
from jax import lax
from jax.experimental import pallas as pl
from jax.experimental.pallas import tpu as pltpu
from jax.sharding import Mesh
from jax.sharding import PartitionSpec as P

DEV = ("dev_0", "dev_1", "dev_2", "dev_3")
GRP_DEV = ("grp", "dev_0", "dev_1", "dev_2", "dev_3")
MESH = pl.DeviceIdType.MESH

epsilon = 1e-06

CHUNKS = 8
WIDTH = 512
IMAGE = 208
ROWS = 416
PATCHES = 196
RING = 4
COLOURS = (("x", "z", "y", 384), ("y", "z", "x", 384), ("z", "x", "y", 256))
FIRST = (0, 384, 768)
LAG = (0, 2, 5, 8, 11, 14, 17, 20)
LATE = CHUNKS + 2
SLOTS = LATE + (LAG[-1] + 2) // 2


def remainder(a, b):
    return lax.rem(a, jnp.int32(b))


def where_on(fixed, half=None):
    index = [slice(None)] * 4
    for axis, at in fixed.items():
        if axis == "x":
            index[0] = at
        elif axis == "y":
            index[2] = at
        else:
            index[1] = remainder(at, 2)
            index[3] = lax.div(at, jnp.int32(2))
    if half is not None:
        axis, part = half
        if axis == "z_lo":
            index[1] = part
        else:
            index[0 if axis == "x" else 2] = pl.ds(2 * part, 2)
    return tuple(index)


HALVES = (("z_lo", "y"), ("z_lo", "x"), ("x", "y"))
HALF_SHAPES = (((4, 2), (2,)), ((4, 2), (2,)), ((2, 4), (2,)))
BLOCK_SHAPES = (((2, 4, 2), (4,)), ((4, 2, 2), (4,)), ((4, 4), (4,)))


def gelu_parts(v):
    twice = 1.0 + lax.erf(v * (1.0 / math.sqrt(2.0)))
    value = 0.5 * v * twice
    slope = 0.5 * twice + v * jnp.exp(-0.5 * v * v) * (1.0 / math.sqrt(2.0 * math.pi))
    return value, slope


def standardized(values):
    centred = values - jnp.mean(values, axis=-1, keepdims=True)
    rstd = lax.rsqrt(jnp.mean(centred * centred, axis=-1, keepdims=True) + epsilon)
    return centred * rstd, rstd


def norm_backward(incoming, scaled, inv_std, gain):
    weighted = incoming * gain
    first_mean = jnp.mean(weighted, axis=-1, keepdims=True)
    second_mean = jnp.mean(weighted * scaled, axis=-1, keepdims=True)
    return inv_std * (weighted - first_mean - scaled * second_mean)


def scratch_of():
    f32, bf16, dma = jnp.float32, jnp.bfloat16, pltpu.SemaphoreType.DMA
    shapes = {}
    for c, (_, _, _, width) in enumerate(COLOURS):
        chunks = CHUNKS + 1 if c == 2 else CHUNKS
        shapes[f"own{c}"] = pltpu.VMEM((4, 2, 4, 2, 2, 8, width), f32)
        shapes[f"sum{c}"] = pltpu.VMEM((chunks, 4, 2, 4, 2, 8, width), f32)
        for p in range(2):
            kept = RING if p == 0 else chunks
            shapes[f"half{c}{p}"] = pltpu.VMEM((kept, 2, *HALF_SHAPES[c][p], 8, width), f32)
            shapes[f"block{c}{p}"] = pltpu.VMEM((kept, 2, *BLOCK_SHAPES[c][p], 8, width), f32)
        shapes[f"last{c}"] = pltpu.VMEM((chunks, 3, 8, width), f32)
    shapes["done"] = pltpu.VMEM((2, CHUNKS, 8, 2 * WIDTH), f32)
    shapes["done_token"] = pltpu.VMEM((2, 8, 256), f32)
    shapes["w_in"] = pltpu.VMEM((2, 1024, WIDTH), bf16)
    shapes["w_out"] = pltpu.VMEM((2, 1024, WIDTH), bf16)
    shapes["act"] = pltpu.VMEM((512, WIDTH), bf16)
    shapes["dhid"] = pltpu.VMEM((512, WIDTH), bf16)
    shapes["hid"] = pltpu.VMEM((512, WIDTH), f32)
    shapes["dact"] = pltpu.VMEM((512, WIDTH), f32)
    shapes["xs"] = pltpu.VMEM((2, IMAGE, 1024), bf16)
    shapes["n1"] = pltpu.VMEM((2, 256, 1024), bf16)
    shapes["act1"] = pltpu.VMEM((2, 512, 1024), bf16)
    shapes["hat2"] = pltpu.VMEM((ROWS, 1024), f32)
    shapes["rstd2"] = pltpu.VMEM((ROWS, 128), f32)
    shapes["n2"] = pltpu.VMEM((512, 1024), bf16)
    shapes["n2t"] = pltpu.VMEM((1024, 512), bf16)
    shapes["cots"] = pltpu.VMEM((512, 1024), bf16)
    shapes["cott"] = pltpu.VMEM((1024, 512), bf16)
    for name in ("tin", "tout"):
        shapes[name] = pltpu.VMEM((512, 256), bf16)
        shapes[name + "t"] = pltpu.VMEM((256, 512), bf16)
        shapes["grad_" + name] = pltpu.VMEM((512, 256), f32)
    shapes["dmr"] = pltpu.VMEM((2, 256, 1024), bf16)
    shapes["dh1"] = pltpu.VMEM((2, 512, 1024), bf16)
    shapes["dn2"] = pltpu.VMEM((ROWS, 1024), f32)
    shapes["columns"] = pltpu.VMEM((256, 128), f32)
    shapes["vector"] = pltpu.VMEM((16, 1024), f32)
    shapes["vector_pair"] = pltpu.VMEM((16, 1024), f32)
    for axis in "xyz":
        shapes["vector_" + axis] = pltpu.VMEM((4, 16, 1024), f32)
    shapes["vector_send"] = dma((3,))
    shapes["vector_recv"] = dma((4, 3))
    shapes["w_sem"] = dma((2, 2))
    shapes["pair_send"] = dma((3,))
    shapes["pair_recv"] = dma((CHUNKS + 1, 3))
    for p in range(2):
        shapes[f"half_send{p}"] = dma((3, 2))
        shapes[f"half_recv{p}"] = dma((CHUNKS + 1, 3, 2))
        shapes[f"block_send{p}"] = dma((3, 2))
        shapes[f"block_recv{p}"] = dma((CHUNKS + 1, 3, 2))
    shapes["last_send"] = dma((3, 3))
    shapes["last_recv"] = dma((CHUNKS + 1, 3, 3))
    shapes["both_send"] = dma((1,))
    shapes["both_recv"] = dma((CHUNKS + 1,))
    return shapes


def block_kernel(names, *refs):
    inputs, cotangent, gain1, shift1, token_in, bias1, token_out, gain2, shift2, win, bias2, wout = refs[:12]
    grad_inputs, grad_tin, grad_tout, grad_in, grad_out, grad_norms, grad_b1, grad_bo, grad_b2 = refs[12:21]
    r = dict(zip(names, refs[21:]))
    f32, bf16 = jnp.float32, jnp.bfloat16
    x, y, core = lax.axis_index("dev_0"), lax.axis_index("dev_2"), lax.axis_index("dev_3")
    high = lax.axis_index("grp")
    me = {"x": x, "y": y, "z": 2 * high + lax.axis_index("dev_1")}

    def device(core=core, **moved):
        at = {**me, **moved}
        return (lax.div(at["z"], jnp.int32(2)), at["x"], remainder(at["z"], 2), at["y"], core)

    def along(axis, by):
        return remainder(me[axis] + by, 4)

    partners = [device(core=1 - core)]
    for axis in ("x", "y", "z"):
        partners += [device(**{axis: along(axis, by)}) for by in (1, 2, 3)]
    barrier = pltpu.get_barrier_semaphore()
    for partner in partners:
        pl.semaphore_signal(barrier, inc=1, device_id=partner, device_id_type=MESH)

    def remote(source, target, send, recv, to):
        return pltpu.make_async_remote_copy(
            src_ref=source, dst_ref=target, send_sem=send, recv_sem=recv, device_id=to, device_id_type=MESH
        )

    def fixed_before(c, p):
        return {axis: me[axis] for axis in COLOURS[c][:p]}

    def colours(j):
        return (2,) if isinstance(j, int) else (0, 1, 2)

    def kept(j, p):
        return remainder(j, RING) if p == 0 else j

    def pair_copies(j):
        every = slice(None)
        return [
            remote(
                r[f"own{c}"].at[every, every, every, 1 - core],
                r[f"sum{c}"].at[j],
                r["pair_send"].at[c],
                r["pair_recv"].at[j, c],
                device(core=1 - core),
            )
            for c in colours(j)
        ]

    def half_copies(j, p):
        copies = []
        for c in colours(j):
            axis = COLOURS[c][p]
            for d, by in enumerate((1, 3)):
                spot = where_on({**fixed_before(c, p), axis: along(axis, 2)}, (HALVES[c][p], d))
                copies.append(
                    remote(
                        r[f"sum{c}"].at[(j, *spot)],
                        r[f"half{c}{p}"].at[kept(j, p), d],
                        r[f"half_send{p}"].at[c, d],
                        r[f"half_recv{p}"].at[j, c, d],
                        device(**{axis: along(axis, by)}),
                    )
                )
        return copies

    def block_copies(j, p):
        copies = []
        for c in colours(j):
            axis = COLOURS[c][p]
            for d, by in enumerate((1, 3)):
                spot = where_on({**fixed_before(c, p), axis: along(axis, by)})
                copies.append(
                    remote(
                        r[f"sum{c}"].at[(j, *spot)],
                        r[f"block{c}{p}"].at[kept(j, p), d],
                        r[f"block_send{p}"].at[c, d],
                        r[f"block_recv{p}"].at[j, c, d],
                        device(**{axis: along(axis, by)}),
                    )
                )
        return copies

    def last_copies(j):
        copies = []
        for c in colours(j):
            axis = COLOURS[c][2]
            for d, by in enumerate((1, 2, 3)):
                spot = where_on({**fixed_before(c, 2), axis: along(axis, by)})
                copies.append(
                    remote(
                        r[f"sum{c}"].at[(j, *spot)],
                        r[f"last{c}"].at[j, d],
                        r["last_send"].at[c, d],
                        r["last_recv"].at[j, c, d],
                        device(**{axis: along(axis, by)}),
                    )
                )
        return copies

    def both_copy(j):
        mine = r["done_token"].at[high] if isinstance(j, int) else r["done"].at[high, j]
        return remote(
            mine,
            mine,
            r["both_send"].at[0],
            r["both_recv"].at[j],
            device(z=along("z", 2)),
        )

    def start(copies):
        for copy in copies:
            copy.start()

    def wait(copies):
        for copy in copies:
            copy.wait()

    def stage(s, j):
        if s == 1:
            wait(pair_copies(j))
            for c in colours(j):
                for b in range(4):
                    r[f"sum{c}"][j, b] += r[f"own{c}"][b, :, :, core]
            start(half_copies(j, 0))
        elif s in (2, 4):
            p = s // 2 - 1
            wait(half_copies(j, p))
            for c in colours(j):
                axis = COLOURS[c][p]
                for d, by in enumerate((1, 3)):
                    spot = where_on({**fixed_before(c, p), axis: along(axis, by)}, (HALVES[c][p], d))
                    r[f"sum{c}"][(j, *spot)] += r[f"half{c}{p}"][kept(j, p), d]
            start(block_copies(j, p))
        elif s in (3, 5):
            p = s // 2 - 1
            wait(block_copies(j, p))
            for c in colours(j):
                spot = where_on(fixed_before(c, p + 1))
                r[f"sum{c}"][(j, *spot)] += r[f"block{c}{p}"][kept(j, p), 0] + r[f"block{c}{p}"][kept(j, p), 1]
            start(half_copies(j, 1) if p == 0 else last_copies(j))
        elif s == 6:
            wait(last_copies(j))
            for c in colours(j):
                width = COLOURS[c][3]
                spot = where_on(me)
                got = r[f"last{c}"]
                total = r[f"sum{c}"][(j, *spot)] + got[j, 0] + (got[j, 1] + got[j, 2])
                if isinstance(j, int):
                    r["done_token"][high] = total
                else:
                    r["done"][high, j, :, FIRST[c] : FIRST[c] + width] = total
            start([both_copy(j)])
        else:
            wait([both_copy(j)])

    def tick(t, parity):
        for s in range(7, 0, -1):
            if (LAG[s] - parity) % 2 == 0:
                j = t - (LAG[s] - parity) // 2

                @pl.when((j >= 0) & (j < CHUNKS))
                def _():
                    stage(s, j)

                @pl.when(j == LATE)
                def _():
                    stage(s, CHUNKS)

    def weights(j):
        slot = remainder(j, 2)
        columns = pl.ds(pl.multiple_of(j * WIDTH, WIDTH), WIDTH)
        return [
            pltpu.make_async_copy(win.at[:, columns], r["w_in"].at[slot], r["w_sem"].at[slot, 0]),
            pltpu.make_async_copy(wout.at[:, columns], r["w_out"].at[slot], r["w_sem"].at[slot, 1]),
        ]

    act, dhid, hid, dact, dn2, vector = r["act"], r["dhid"], r["hid"], r["dact"], r["dn2"], r["vector"]

    def blocks_of(count, size, step, start_with=0):
        def at_block(i, carry):
            return step(pl.ds(pl.multiple_of(i * size, size), size), i, carry)

        return lax.fori_loop(0, count, at_block, start_with)

    def real(i):
        return lax.broadcasted_iota(jnp.int32, (16, 1), 0) + 16 * i < PATCHES

    def folded(values):
        return jnp.sum(values.reshape(2, 8, 1024), axis=0)

    def token_hidden(b, columns):
        hid[...] = jnp.dot(r["tin"][...], r["n1"][b, :, columns], preferred_element_type=f32)

    def prologue():
        for name, ref in (("tin", token_in), ("tout", token_out)):
            r[name][...] = jnp.zeros((512, 256), bf16)
            r[name][:, :PATCHES] = ref[...]
            r[name + "t"][...] = r[name][...].T
        for b in range(2):
            tail = jnp.zeros((256 - IMAGE, 1024), bf16)
            r["xs"][b, 192:, :] = jnp.zeros((16, 1024), bf16)
            r["xs"][b, :PATCHES, :] = inputs[b]
            r["cots"][IMAGE * b + 192 : IMAGE * b + 208, :] = jnp.zeros((16, 1024), bf16)
            r["cots"][IMAGE * b : IMAGE * b + PATCHES, :] = cotangent[b]
            r["n1"][b, IMAGE:, :] = tail
            r["dmr"][b, IMAGE:, :] = tail

            def first_norm(at, i, _):
                hat, _rstd = standardized(r["xs"][b, at, :].astype(f32))
                value = hat * gain1[...] + shift1[...]
                r["n1"][b, at, :] = jnp.where(real(i), value, 0.0).astype(bf16)
                return 0

            blocks_of(IMAGE // 16, 16, first_norm)
        r["cots"][ROWS:, :] = jnp.zeros((512 - ROWS, 1024), bf16)
        r["n2"][ROWS:, :] = jnp.zeros((512 - ROWS, 1024), bf16)
        r["cott"][...] = r["cots"][...].T
        for b in range(2):
            for half in range(2):
                columns = slice(512 * half, 512 * (half + 1))
                token_hidden(b, columns)

                def activate(at, i, _):
                    value = gelu_parts(hid[at, :] + bias1[at, :])[0]
                    r["act1"][b, at, columns] = value.astype(bf16)
                    return 0

                blocks_of(16, 32, activate)
            for q in range(4):
                columns = slice(256 * q, 256 * (q + 1))
                r["hat2"][IMAGE * b : IMAGE * (b + 1), columns] = jnp.dot(
                    r["toutt"][:IMAGE, :], r["act1"][b, :, columns], preferred_element_type=f32
                )

            def second_norm(at, i, _):
                rows = pl.ds(pl.multiple_of(IMAGE * b + 16 * i, 16), 16)
                hat, rstd = standardized(r["xs"][b, at, :].astype(f32) + r["hat2"][rows, :])
                r["hat2"][rows, :] = hat
                r["rstd2"][rows, :] = jnp.broadcast_to(rstd, (16, 128))
                value = hat * gain2[...] + shift2[...]
                r["n2"][rows, :] = jnp.where(real(i), value, 0.0).astype(bf16)
                return 0

            blocks_of(IMAGE // 16, 16, second_norm)
        r["n2t"][...] = r["n2"][...].T

    def forward(j):
        slot = remainder(j, 2)
        wait(weights(j))

        @pl.when(j + 1 < CHUNKS)
        def _():
            start(weights(j + 1))

        columns = pl.ds(pl.multiple_of(j * WIDTH, WIDTH), WIDTH)
        for b in range(WIDTH // 256):
            part = slice(256 * b, 256 * (b + 1))
            hid[:ROWS, part] = jnp.dot(r["n2"][:ROWS, :], r["w_in"][slot, :, part], preferred_element_type=f32)
            dact[:ROWS, part] = jnp.dot(r["cots"][:ROWS, :], r["w_out"][slot, :, part], preferred_element_type=f32)
        shift = bias2[:, columns]

        def rows(at, i, total):
            value, slope = gelu_parts(hid[at, :] + shift)
            act[at, :] = value.astype(bf16)
            d = (dact[at, :] * slope).astype(bf16)
            dhid[at, :] = d
            return total + jnp.sum(d.astype(f32).reshape(4, 8, WIDTH), axis=0)

        total = blocks_of(ROWS // 32, 32, rows, jnp.zeros((8, WIDTH), f32))
        half = pl.ds(pl.multiple_of(remainder(j, 2) * WIDTH, WIDTH), WIDTH)
        vector[pl.ds(5 + lax.div(j, jnp.int32(2)), 1), half] = jnp.sum(total, axis=0, keepdims=True)

    def gradients(j):
        slot = remainder(j, 2)

        def rows(at, i, _):
            out = jnp.dot(r["cott"][at, :], act[...], preferred_element_type=f32).reshape(2, 4, 2, 2, 8, WIDTH)
            r["own0"][i] = out[..., :384]
            r["own1"][i, :, :, :, :, :, :128] = out[..., 384:]
            inn = jnp.dot(r["n2t"][at, :], dhid[...], preferred_element_type=f32).reshape(2, 4, 2, 2, 8, WIDTH)
            r["own1"][i, :, :, :, :, :, 128:] = inn[..., :256]
            r["own2"][i] = inn[..., 256:]
            return 0

        blocks_of(4, 256, rows)
        start(pair_copies(j))
        for b in range(4):
            part = slice(256 * b, 256 * (b + 1))
            dn2[:, part] += lax.dot_general(
                dhid[:ROWS, :],
                r["w_in"][slot, part, :],
                (((1,), (1,)), ((), ())),
                preferred_element_type=f32,
            )

    def across(a, b):
        return lax.dot_general(a, b, (((1,), (1,)), ((), ())), preferred_element_type=f32)

    def token_backward(b):
        def second_norm(at, i, sums):
            rows = pl.ds(pl.multiple_of(IMAGE * b + 16 * i, 16), 16)
            hat, incoming = r["hat2"][rows, :], dn2[rows, :]
            g = r["cots"][rows, :].astype(f32)
            dmixed = g + norm_backward(incoming, hat, r["rstd2"][rows, :1], gain2[...])
            dn2[rows, :] = dmixed
            r["dmr"][b, at, :] = dmixed.astype(bf16)
            r["columns"][at, :] += jnp.broadcast_to(jnp.sum(dmixed, axis=1, keepdims=True), (16, 128))
            return (sums[0] + folded(incoming * hat), sums[1] + folded(incoming), sums[2] + folded(g))

        zero = jnp.zeros((8, 1024), f32)
        sums = blocks_of(IMAGE // 16, 16, second_norm, (zero, zero, zero))
        for row, total in zip((2, 3, 4), sums):
            vector[row : row + 1, :] += jnp.sum(total, axis=0, keepdims=True)
        for half in range(2):
            columns = slice(512 * half, 512 * (half + 1))
            token_hidden(b, columns)
            dact[...] = jnp.dot(r["tout"][...], r["dmr"][b, :, columns], preferred_element_type=f32)

            def back(at, i, _):
                slope = gelu_parts(hid[at, :] + bias1[at, :])[1]
                r["dh1"][b, at, columns] = (dact[at, :] * slope).astype(bf16)
                return 0

            blocks_of(16, 32, back)

    def token_gradients(b):
        r["grad_tin"][...] += across(r["dh1"][b], r["n1"][b])
        r["grad_tout"][...] += across(r["act1"][b], r["dmr"][b])
        ones = jnp.ones((8, 1024), bf16)
        vector[9:10, :512] += across(ones, r["dh1"][b])[:1]

    def send_token_gradients():
        for h, name in enumerate(("grad_tin", "grad_tout")):
            r["own2"][:, :, :, :, h] = r[name][...].reshape(4, 2, 4, 2, 8, 256)
        start(pair_copies(CHUNKS))

    def input_gradients(b):
        for half in range(2):
            columns = slice(512 * half, 512 * (half + 1))
            hid[:IMAGE, :] = jnp.dot(r["tint"][:IMAGE, :], r["dh1"][b, :, columns], preferred_element_type=f32)
            r["hat2"][:IMAGE, columns] = hid[:IMAGE, :]

        def first_norm(at, i, sums):
            hat, rstd = standardized(r["xs"][b, at, :].astype(f32))
            incoming = r["hat2"][at, :]
            rows = pl.ds(pl.multiple_of(IMAGE * b + 16 * i, 16), 16)
            total = dn2[rows, :] + norm_backward(incoming, hat, rstd, gain1[...])
            r["xs"][b, at, :] = total.astype(bf16)
            return (sums[0] + folded(incoming * hat), sums[1] + folded(incoming))

        zero = jnp.zeros((8, 1024), f32)
        sums = blocks_of(IMAGE // 16, 16, first_norm, (zero, zero))
        for row, total in zip((0, 1), sums):
            vector[row : row + 1, :] += jnp.sum(total, axis=0, keepdims=True)

    def vector_copies(step):
        if step == 0:
            return [
                remote(
                    vector, r["vector_pair"], r["vector_send"].at[0], r["vector_recv"].at[0, 0], device(core=1 - core)
                )
            ]
        axis = "xyz"[step - 1]
        at = r["vector_" + axis]
        return [
            remote(
                at.at[0],
                at.at[by],
                r["vector_send"].at[by - 1],
                r["vector_recv"].at[step, by - 1],
                device(**{axis: along(axis, by)}),
            )
            for by in (1, 2, 3)
        ]

    def vector_total(axis):
        at = r["vector_" + axis]
        terms = [at[remainder(me[axis] + 4 - k, 4)] for k in range(4)]
        return (terms[0] + terms[1]) + (terms[2] + terms[3])

    def vector_stage(step):
        if step == 0:
            vector[9:10, 512:768] = r["columns"][...].T[:1, :]
            start(vector_copies(0))
            return
        wait(vector_copies(step - 1))
        total = vector[...] + r["vector_pair"][...] if step == 1 else vector_total("xyz"[step - 2])
        if step < 4:
            r["vector_" + "xyz"[step - 1]][0] = total
            start(vector_copies(step))
        else:
            grad_norms[...] = total[:5]
            for k in range(4):
                grad_b2[:, 1024 * k : 1024 * (k + 1)] = total[5 + k : 6 + k]
            grad_b1[...] = total[9:10, :512]
            grad_bo[...] = total[9:10, 512 : 512 + PATCHES]

    start(weights(jnp.int32(0)))
    for name in ("act", "dhid"):
        r[name][ROWS:, :] = jnp.zeros((512 - ROWS, WIDTH), bf16)
    for name in ("dn2", "vector", "columns", "grad_tin", "grad_tout"):
        r[name][...] = jnp.zeros(r[name].shape, f32)
    prologue()
    pl.semaphore_wait(barrier, len(partners))

    def slot_of(t, _):
        @pl.when(t < CHUNKS)
        def _():
            forward(t)

        @pl.when((t >= CHUNKS) & (t < CHUNKS + 2))
        def _():
            token_backward(t - CHUNKS)

        @pl.when(t == CHUNKS + 2)
        def _():
            input_gradients(0)

        tick(t, 0)

        @pl.when(t < CHUNKS)
        def _():
            gradients(t)

        @pl.when((t >= CHUNKS) & (t < CHUNKS + 2))
        def _():
            token_gradients(t - CHUNKS)

        @pl.when(t == CHUNKS + 1)
        def _():
            send_token_gradients()

        @pl.when(t == CHUNKS + 2)
        def _():
            input_gradients(1)
            vector_stage(0)

        tick(t, 1)

        for step in range(1, 5):

            @pl.when(t == CHUNKS + 2 + step)
            def _():
                vector_stage(step)

        return 0

    lax.fori_loop(0, SLOTS, slot_of, 0)
    for b in range(2):
        grad_inputs[b] = r["xs"][b, :PATCHES, :]
    for h in range(2):
        for j in range(CHUNKS):
            for g, out in enumerate((grad_out, grad_in)):
                out[8 * h : 8 * (h + 1), WIDTH * j : WIDTH * (j + 1)] = r["done"][
                    h, j, :, WIDTH * g : WIDTH * (g + 1)
                ]
    grad_tin[...] = r["done_token"][0, :, :PATCHES]
    grad_tout[...] = r["done_token"][1, :, :PATCHES]


def per_device(
    inputs,
    cotangent,
    first_gain,
    first_shift,
    token_in,
    token_in_bias,
    token_out,
    second_gain,
    second_shift,
    channel_in,
    channel_in_bias,
    channel_out,
):
    f32 = jnp.float32
    hidden = channel_in.shape[1]
    shapes = scratch_of()
    names = tuple(shapes)
    vmem, anywhere = pl.BlockSpec(memory_space=pltpu.VMEM), pl.BlockSpec(memory_space=pl.ANY)

    def kernel(*refs):
        block_kernel(names, *refs)

    results = pl.pallas_call(
        kernel,
        out_shape=(
            jax.ShapeDtypeStruct(inputs.shape, jnp.bfloat16),
            jax.ShapeDtypeStruct((8, PATCHES), f32),
            jax.ShapeDtypeStruct((8, PATCHES), f32),
            jax.ShapeDtypeStruct((16, hidden), f32),
            jax.ShapeDtypeStruct((16, hidden), f32),
            jax.ShapeDtypeStruct((5, 1024), f32),
            jax.ShapeDtypeStruct((1, 512), f32),
            jax.ShapeDtypeStruct((1, PATCHES), f32),
            jax.ShapeDtypeStruct((1, hidden), f32),
        ),
        in_specs=[vmem] * 9 + [anywhere, vmem, anywhere],
        out_specs=(vmem,) * 9,
        scratch_shapes=list(shapes.values()),
        compiler_params=pltpu.CompilerParams(collective_id=0, has_side_effects=True, vmem_limit_bytes=67_000_000),
        name="block_backward",
    )(
        inputs,
        cotangent,
        first_gain.reshape(1, -1),
        first_shift.reshape(1, -1),
        token_in,
        token_in_bias.reshape(-1, 1),
        token_out,
        second_gain.reshape(1, -1),
        second_shift.reshape(1, -1),
        channel_in,
        channel_in_bias.reshape(1, -1),
        channel_out,
    )
    return (*results[:6], *(a[0] for a in results[6:]))


def solution(mesh):
    split = Mesh(
        mesh.devices.reshape(mesh.shape["grp"], 4, 2, 4, 2),
        ("grp", "dev_0", "dev_1", "dev_2", "dev_3"),
    )
    in_specs = (
        P(GRP_DEV, None, None),
        P(GRP_DEV, None, None),
        P(),
        P(),
        P(),
        P(),
        P(),
        P(),
        P(),
        P(),
        P(),
        P(),
    )
    out_specs = (
        P(GRP_DEV, None, None),
        P(DEV, None),
        P(DEV, None),
        P(DEV, None),
        P(DEV, None),
        P(),
        P(),
        P(),
        P(),
    )
    return jax.shard_map(
        per_device, mesh=split, in_specs=in_specs, out_specs=out_specs, check_vma=False
    )
```

time: 236 us -> 157 us (0.67)
  blocking collectives: 64.6 us -> 0 us
  Pallas kernels: 104 us -> 132 us
  other arithmetic: 13.3 us -> 0 us
  matrix products: 11.3 us -> 0 us
  starting transfers between devices: 9.63 us -> 0 us
  waiting for transfers between devices: 7.68 us -> 0 us
    psum x1 -> x0, blocking collectives: 64.6 us -> none  [together_2(): running = lax.psum(jnp.concatenate([a.ravel() for a in arrays]), axis)]
    pallas_call x1, Pallas kernels: 104 us -> 132 us  [per_device(): pl.pallas_call(kernel, out_shape=(jax.ShapeDtypeStruct(inputs.shape, jnp....]
    unnamed x46 -> x13, local copies, waits for them, and re-layouts: 7.74 us -> 22 us
    dot_general x6 -> x0, matrix products: 11.3 us -> none  [the longest x1 3.73 us: per_device(): jnp.einsum('bcs,sp->bpc', dhidden1, token_in, preferred_element_type=f32)]
    reduce_sum x9 -> x0, other arithmetic: 10.8 us -> none  [the longest x1 2.85 us: per_device(): jnp.sum(dnormed2, axis=(0, 1))]
    all_to_all x2 -> x0, starting transfers between devices: 9.63 us -> none  [the longest x1 6.38 us: summed_on_arrival(): lax.all_to_all(cut_along(shard, dim, count), axis, 0, 0, tiled=True)]
    all_to_all x2 -> x0, waiting for transfers between devices: 7.68 us -> none  [the longest x1 7.68 us: summed_on_arrival(): lax.all_to_all(cut_along(shard, dim, count), axis, 0, 0, tiled=True)]
    pad x4 -> x0, local copies, waits for them, and re-layouts: 4.16 us -> none  [the longest x2 2.22 us: channel_stage(): across = lambda a: jnp.pad(a.T, ((0, 0), (0, 512 - tokens)))]
  transfers between devices with their start and end apart: 2 -> 0, of which waited for: 1 -> 0; matrix products, arithmetic and copies ran while one was open for 6% -> 0% of each run, Pallas kernels for 0% -> 0%
where the time goes in v2:
time: 157 us
  Pallas kernels  132 us (84%)
  local copies, waits for them, and re-layouts  23.5 us (15%)
    pallas_call x1, Pallas kernels, per_device(): pl.pallas_call(kernel, out_shape=(jax.ShapeDtypeStruct(inputs.shape, jnp....  132 us
    unnamed x13, local copies, waits for them, and re-layouts  22 us

profile of v2, /device:TPU:0, one launch (start us, length us, event | category | flops | bytes accessed | tf_op | source)
XLA Modules:
  0.0 156.6 jit_solution(7177083816031680878)
XLA Ops:
  0.6 1.8 %copy.28.refs_4_ = bf16[512,196]{1,0:T(8,128)(2,1)} copy(bf16[512,196]{0,1:T(8,128)(2,1)} %param.16) | data formatting | bytes 401408 | tf_op args[4]
  2.4 1.5 copy.29.refs_5_
  3.9 1.8 %copy.30.refs_6_ = bf16[512,196]{1,0:T(8,128)(2,1)} copy(bf16[512,196]{0,1:T(8,128)(2,1)} %param.18) | data formatting | bytes 401408 | tf_op args[6]
  5.7 2.2 %copy.26.refs_0_ = bf16[2,196,1024]{2,1,0:T(8,128)(2,1)} copy(bf16[2,196,1024]{2,0,1:T(2,128)(2,1)} %param.12) | data formatting | bytes 1605632 | tf_op args[0]
  8.0 2.3 %copy.27.refs_1_ = bf16[2,196,1024]{2,1,0:T(8,128)(2,1)} copy(bf16[2,196,1024]{2,0,1:T(2,128)(2,1)} %param.13) | data formatting | bytes 1605632 | tf_op args[1]
  10.2 132.4 %block_backward.1 = (bf16[2,196,1024]{2,1,0:T(8,128)(2,1)}, f32[8,196]{1,0:T(8,128)}, f32[8,196]{1,0:T(8,128)}, f32[16,4096]{1,0:T(8,128)}, f32[16,4096]{1,0:T(8...) custom-call(bf16[2,196,1024]{2,1,0:T(8,128)(2,1)} %copy.26.refs_0_, ...), custom_call_target="tpu_custom_call" | custom-call | tf_op jit(solution)/shard_map/block_backward/pallas_call | solution.py:621
  142.7 2.9 %copy.31 = bf16[2,196,1024]{2,0,1:T(2,128)(2,1)} copy(bf16[2,196,1024]{2,1,0:T(8,128)(2,1)} %get-tuple-element.36) | data formatting | bytes 1605632
  145.5 1.3 copy.40
  146.8 1.3 copy.41
  148.1 1.7 %copy.42 = f32[16,4096]{1,0:T(8,128)} copy(f32[16,4096]{1,0:T(8,128)} %get-tuple-element.57) | data formatting | bytes 524288
  149.8 1.7 %copy.43 = f32[16,4096]{1,0:T(8,128)} copy(f32[16,4096]{1,0:T(8,128)} %get-tuple-element.58) | data formatting | bytes 524288
  151.4 1.4 copy.44
  152.8 1.2 copy.45
  154.1 1.2 copy.46
  155.3 1.3 copy.47

commit v3 on v2

v3 whole, which is shorter than its diff:
```python
import math
from typing import Any, NamedTuple

import jax
import jax.numpy as jnp
from jax import lax
from jax.experimental import pallas as pl
from jax.experimental.pallas import tpu as pltpu
from jax.sharding import Mesh
from jax.sharding import PartitionSpec as P

DEV = ("dev_0", "dev_1", "dev_2", "dev_3")
GRP_DEV = ("grp", "dev_0", "dev_1", "dev_2", "dev_3")
MESH = pl.DeviceIdType.MESH

epsilon = 1e-06

AXES = ("x", "y", "z")
CHUNKS = 8
WIDTH = 512
IMAGE = 208
ROWS = 416
PATCHES = 196
COLOURS = (("x", "z", "y", 384), ("y", "z", "x", 384), ("z", "x", "y", 256))
FIRST = (0, 384, 768)
LAG = (0, 0, 2, 4, 6, 8, 10, 12)
LATE = 14
LATE_LAG = (0, 0, 1, 3, 4, 5, 6, 7)
PIECES = CHUNKS + 6
SLOTS = 2 * (CHUNKS - 1) + LAG[-1] + 1
EARLY_SUMS = CHUNKS + 3
LATE_SUMS = CHUNKS + 6


def remainder(a, b):
    return lax.rem(a, jnp.int32(b))


def where_on(fixed, half=None):
    index = [slice(None)] * 4
    for axis, at in fixed.items():
        if axis == "x":
            index[0] = at
        elif axis == "y":
            index[2] = at
        else:
            index[1] = remainder(at, 2)
            index[3] = lax.div(at, jnp.int32(2))
    if half is not None:
        axis, part = half
        if axis == "z_lo":
            index[1] = part
        else:
            index[0 if axis == "x" else 2] = pl.ds(2 * part, 2)
    return tuple(index)


HALVES = (("z_lo", "y"), ("z_lo", "x"), ("x", "y"))
HALF_SHAPES = (((4, 2), (2,)), ((4, 2), (2,)), ((2, 4), (2,)))
BLOCK_SHAPES = (((2, 4, 2), (4,)), ((4, 2, 2), (4,)), ((4, 4), (4,)))


def gelu_parts(v):
    twice = 1.0 + lax.erf(v * (1.0 / math.sqrt(2.0)))
    value = 0.5 * v * twice
    slope = 0.5 * twice + v * jnp.exp(-0.5 * v * v) * (1.0 / math.sqrt(2.0 * math.pi))
    return value, slope


def standardized(values):
    centred = values - jnp.mean(values, axis=-1, keepdims=True)
    rstd = lax.rsqrt(jnp.mean(centred * centred, axis=-1, keepdims=True) + epsilon)
    return centred * rstd, rstd


def norm_backward(incoming, scaled, inv_std, gain):
    weighted = incoming * gain
    first_mean = jnp.mean(weighted, axis=-1, keepdims=True)
    second_mean = jnp.mean(weighted * scaled, axis=-1, keepdims=True)
    return inv_std * (weighted - first_mean - scaled * second_mean)


class Scratch(NamedTuple):
    own: Any
    sums: Any
    half: Any
    block: Any
    last: Any
    done: Any
    done_token: Any
    w_in: Any
    w_out: Any
    act: Any
    dhid: Any
    hid: Any
    dact: Any
    xs: Any
    n1: Any
    act1: Any
    hat2: Any
    rstd2: Any
    n2: Any
    n2t: Any
    cots: Any
    cott: Any
    tin: Any
    tint: Any
    tout: Any
    toutt: Any
    grad_tin: Any
    grad_tout: Any
    dn2: Any
    columns: Any
    bias1: Any
    early: Any
    late: Any
    w_sem: Any
    pair_send: Any
    pair_recv: Any
    half_send: Any
    half_recv: Any
    block_send: Any
    block_recv: Any
    last_send: Any
    last_recv: Any
    both_send: Any
    both_recv: Any
    sums_send: Any
    sums_recv: Any


def scratch_of():
    f32 = lambda *shape: pltpu.VMEM(shape, jnp.float32)
    bf16 = lambda *shape: pltpu.VMEM(shape, jnp.bfloat16)
    dma = lambda *shape: pltpu.SemaphoreType.DMA(shape)
    widths = [colour[3] for colour in COLOURS]
    chunks = [CHUNKS, CHUNKS, CHUNKS + 1]

    def received(shapes):
        return [
            [f32(chunks[c], 2, *shapes[c][p], 8, widths[c]) for p in range(2)] for c in range(3)
        ]

    return Scratch(
        own=[f32(4, 2, 4, 2, 2, 8, w) for w in widths],
        sums=[f32(chunks[c], 4, 2, 4, 2, 8, widths[c]) for c in range(3)],
        half=received(HALF_SHAPES),
        block=received(BLOCK_SHAPES),
        last=[f32(chunks[c], 3, 8, widths[c]) for c in range(3)],
        done=f32(2, CHUNKS, 8, 2 * WIDTH),
        done_token=f32(2, 8, 256),
        w_in=bf16(2, 1024, WIDTH),
        w_out=bf16(2, 1024, WIDTH),
        act=bf16(512, WIDTH),
        dhid=bf16(512, WIDTH),
        hid=f32(512, WIDTH),
        dact=f32(512, WIDTH),
        xs=bf16(2, IMAGE, 1024),
        n1=bf16(2, 256, 1024),
        act1=bf16(2, 512, 1024),
        hat2=f32(ROWS, 1024),
        rstd2=f32(ROWS, 128),
        n2=bf16(512, 1024),
        n2t=bf16(1024, 512),
        cots=bf16(512, 1024),
        cott=bf16(1024, 512),
        tin=bf16(512, 256),
        tint=bf16(256, 512),
        tout=bf16(512, 256),
        toutt=bf16(256, 512),
        grad_tin=f32(512, 256),
        grad_tout=f32(512, 256),
        dn2=f32(ROWS, 1024),
        columns=f32(256, 128),
        bias1=f32(512, 128),
        early=[f32(8, 1024), f32(8, 1024), *(f32(4, 8, 1024) for _ in AXES)],
        late=[f32(8, 384), f32(8, 384), *(f32(4, 8, 384) for _ in AXES)],
        w_sem=dma(2, 2),
        pair_send=dma(CHUNKS + 1, 3),
        pair_recv=dma(CHUNKS + 1, 3),
        half_send=[dma(CHUNKS + 1, 3, 2) for _ in range(2)],
        half_recv=[dma(CHUNKS + 1, 3, 2) for _ in range(2)],
        block_send=[dma(CHUNKS + 1, 3, 2) for _ in range(2)],
        block_recv=[dma(CHUNKS + 1, 3, 2) for _ in range(2)],
        last_send=dma(CHUNKS + 1, 3, 3),
        last_recv=dma(CHUNKS + 1, 3, 3),
        both_send=dma(CHUNKS + 1),
        both_recv=dma(CHUNKS + 1),
        sums_send=dma(2, 4, 3),
        sums_recv=dma(2, 4, 3),
    )


def block_kernel(*refs):
    inputs, cotangent, gain1, shift1, token_in, bias1, token_out, gain2, shift2, win, bias2, wout = refs[:12]
    grad_inputs, grad_tin, grad_tout, grad_in, grad_out, grad_norms, grad_b1, grad_bo, grad_b2 = refs[12:21]
    r = refs[21]
    f32, bf16 = jnp.float32, jnp.bfloat16
    x, y, core = lax.axis_index("dev_0"), lax.axis_index("dev_2"), lax.axis_index("dev_3")
    high = lax.axis_index("grp")
    me = {"x": x, "y": y, "z": 2 * high + lax.axis_index("dev_1")}

    def device(core=core, **moved):
        at = {**me, **moved}
        return (lax.div(at["z"], jnp.int32(2)), at["x"], remainder(at["z"], 2), at["y"], core)

    def along(axis, by):
        return remainder(me[axis] + by, 4)

    partners = [device(core=1 - core)]
    for axis in AXES:
        partners += [device(**{axis: along(axis, by)}) for by in (1, 2, 3)]
    barrier = pltpu.get_barrier_semaphore()
    for partner in partners:
        pl.semaphore_signal(barrier, inc=1, device_id=partner, device_id_type=MESH)

    def remote(source, target, send, recv, to):
        return pltpu.make_async_remote_copy(
            src_ref=source, dst_ref=target, send_sem=send, recv_sem=recv, device_id=to, device_id_type=MESH
        )

    def fixed_before(c, p):
        return {axis: me[axis] for axis in COLOURS[c][:p]}

    def colours(j):
        return (2,) if isinstance(j, int) else (0, 1, 2)

    def pair_copies(j):
        every = slice(None)
        return [
            remote(
                r.own[c].at[every, every, every, 1 - core],
                r.sums[c].at[j],
                r.pair_send.at[j, c],
                r.pair_recv.at[j, c],
                device(core=1 - core),
            )
            for c in colours(j)
        ]

    def half_copies(j, p):
        copies = []
        for c in colours(j):
            axis = COLOURS[c][p]
            for d, by in enumerate((1, 3)):
                spot = where_on({**fixed_before(c, p), axis: along(axis, 2)}, (HALVES[c][p], d))
                copies.append(
                    remote(
                        r.sums[c].at[(j, *spot)],
                        r.half[c][p].at[j, d],
                        r.half_send[p].at[j, c, d],
                        r.half_recv[p].at[j, c, d],
                        device(**{axis: along(axis, by)}),
                    )
                )
        return copies

    def block_copies(j, p):
        copies = []
        for c in colours(j):
            axis = COLOURS[c][p]
            for d, by in enumerate((1, 3)):
                spot = where_on({**fixed_before(c, p), axis: along(axis, by)})
                copies.append(
                    remote(
                        r.sums[c].at[(j, *spot)],
                        r.block[c][p].at[j, d],
                        r.block_send[p].at[j, c, d],
                        r.block_recv[p].at[j, c, d],
                        device(**{axis: along(axis, by)}),
                    )
                )
        return copies

    def last_copies(j):
        copies = []
        for c in colours(j):
            axis = COLOURS[c][2]
            for d, by in enumerate((1, 2, 3)):
                spot = where_on({**fixed_before(c, 2), axis: along(axis, by)})
                copies.append(
                    remote(
                        r.sums[c].at[(j, *spot)],
                        r.last[c].at[j, d],
                        r.last_send.at[j, c, d],
                        r.last_recv.at[j, c, d],
                        device(**{axis: along(axis, by)}),
                    )
                )
        return copies

    def both_copy(j):
        mine = r.done_token.at[high] if isinstance(j, int) else r.done.at[high, j]
        return remote(
            mine,
            mine,
            r.both_send.at[j],
            r.both_recv.at[j],
            device(z=along("z", 2)),
        )

    def start(copies):
        for copy in copies:
            copy.start()

    def wait(copies):
        for copy in copies:
            copy.wait()

    def stage(s, j):
        if s == 1:
            wait(pair_copies(j))
            for c in colours(j):
                for b in range(4):
                    r.sums[c][j, b] += r.own[c][b, :, :, core]
            start(half_copies(j, 0))
        elif s in (2, 4):
            p = s // 2 - 1
            wait(half_copies(j, p))
            for c in colours(j):
                axis = COLOURS[c][p]
                for d, by in enumerate((1, 3)):
                    spot = where_on({**fixed_before(c, p), axis: along(axis, by)}, (HALVES[c][p], d))
                    r.sums[c][(j, *spot)] += r.half[c][p][j, d]
            start(block_copies(j, p))
        elif s in (3, 5):
            p = s // 2 - 1
            wait(block_copies(j, p))
            for c in colours(j):
                spot = where_on(fixed_before(c, p + 1))
                r.sums[c][(j, *spot)] += r.block[c][p][j, 0] + r.block[c][p][j, 1]
            start(half_copies(j, 1) if p == 0 else last_copies(j))
        elif s == 6:
            wait(last_copies(j))
            for c in colours(j):
                width = COLOURS[c][3]
                spot = where_on(me)
                got = r.last[c]
                total = r.sums[c][(j, *spot)] + got[j, 0] + (got[j, 1] + got[j, 2])
                if isinstance(j, int):
                    r.done_token[high] = total
                else:
                    r.done[high, j, :, FIRST[c] : FIRST[c] + width] = total
            start([both_copy(j)])
        else:
            wait([both_copy(j)])

    def serve(t):
        for s in range(7, 1, -1):
            from_start = t - LAG[s]
            j = lax.div(from_start, jnp.int32(2))

            @pl.when((from_start >= 0) & (from_start < 2 * CHUNKS) & (remainder(from_start + 2 * CHUNKS, 2) == 0))
            def _():
                stage(s, j)

            @pl.when(t == LATE + LATE_LAG[s])
            def _():
                stage(s, CHUNKS)

    def weights(j):
        slot = remainder(j, 2)
        columns = pl.ds(pl.multiple_of(j * WIDTH, WIDTH), WIDTH)
        return [
            pltpu.make_async_copy(win.at[:, columns], r.w_in.at[slot], r.w_sem.at[slot, 0]),
            pltpu.make_async_copy(wout.at[:, columns], r.w_out.at[slot], r.w_sem.at[slot, 1]),
        ]

    act, dhid, hid, dact, dn2 = r.act, r.dhid, r.hid, r.dact, r.dn2
    early, late = r.early[0], r.late[0]

    def blocks_of(count, size, step, carry=0, group=1):
        def at_block(i, carry):
            for u in range(group):
                n = i * group + u
                carry = step(pl.ds(pl.multiple_of(n * size, size), size), n, carry)
            return carry

        carry = lax.fori_loop(0, count // group, at_block, carry)
        for n in range(count // group * group, count):
            carry = step(pl.ds(n * size, size), n, carry)
        return carry

    def real(i):
        return lax.broadcasted_iota(jnp.int32, (16, 1), 0) + 16 * i < PATCHES

    def folded(values):
        return jnp.sum(values.reshape(2, 8, 1024), axis=0)

    def rows_of(b, i):
        return pl.ds(pl.multiple_of(IMAGE * b + 16 * i, 16), 16)

    def columns_of(half):
        return slice(512 * half, 512 * (half + 1))

    def dh1(b, half):
        return r.w_in.at[b, columns_of(half), :]

    def dmr(b, half):
        return r.w_out.at[b, 256 * half : 256 * (half + 1), :]

    def token_hidden(b, columns):
        hid[...] = jnp.dot(r.tin[...], r.n1[b, :, columns], preferred_element_type=f32)

    def both_images(ref, i, whole=True):
        if whole:
            values = ref[pl.ds(pl.multiple_of(16 * i, 16), 16)].astype(f32)
            return [values[:, b, :] for b in range(2)]
        values = ref[192:PATCHES].astype(f32)
        blocks = []
        for b in range(2):
            spot = r.hat2.at[16 * b : 16 * (b + 1), :]
            spot[...] = jnp.zeros((16, 1024), f32)
            spot[: PATCHES - 192, :] = values[:, b, :]
            blocks.append(spot[...])
        return blocks

    def prologue():
        for direct, turned, ref in ((r.tin, r.tint, token_in), (r.tout, r.toutt, token_out)):
            turned[192:, :] = jnp.zeros((64, 512), bf16)
            turned[:PATCHES, :] = ref[...]
            direct[...] = turned[...].T
        r.bias1[...] = jnp.broadcast_to(bias1[...], (128, 512)).T
        for b in range(2):
            r.n1[b, IMAGE:, :] = jnp.zeros((256 - IMAGE, 1024), bf16)
        gain, shift = gain1[...], shift1[...]

        def first_norm(at, i, _, whole=True):
            for b, values in enumerate(both_images(inputs, i, whole)):
                r.xs[b, at, :] = values.astype(bf16)
                value = standardized(values)[0] * gain + shift
                r.n1[b, at, :] = (value if whole else jnp.where(real(i), value, 0.0)).astype(bf16)
            return 0

        blocks_of(12, 16, first_norm, group=3)
        first_norm(pl.ds(192, 16), 12, 0, False)

        def split(at, i, _, whole=True):
            for b, values in enumerate(both_images(cotangent, i, whole)):
                r.cots[rows_of(b, i), :] = values.astype(bf16)
            return 0

        blocks_of(12, 16, split, group=3)
        split(None, 12, 0, False)
        r.cots[ROWS:, :] = jnp.zeros((512 - ROWS, 1024), bf16)
        r.n2[ROWS:, :] = jnp.zeros((512 - ROWS, 1024), bf16)
        for b in range(2):
            for half in range(2):
                columns = columns_of(half)
                token_hidden(b, columns)

                def activate(at, i, _):
                    value = gelu_parts(hid[at, :] + r.bias1[at, :1])[0]
                    r.act1[b, at, columns] = value.astype(bf16)
                    return 0

                blocks_of(16, 32, activate, group=2)
            for half in range(2):
                columns = columns_of(half)
                r.hat2[IMAGE * b : IMAGE * (b + 1), columns] = jnp.dot(
                    r.toutt[:IMAGE, :], r.act1[b, :, columns], preferred_element_type=f32
                )
        r.cott[...] = r.cots[...].T
        gain, shift = gain2[...], shift2[...]

        def second_norm(at, i, _):
            for b in range(2):
                rows = rows_of(b, i)
                hat, rstd = standardized(r.xs[b, at, :].astype(f32) + r.hat2[rows, :])
                r.hat2[rows, :] = hat
                r.rstd2[rows, :] = jnp.broadcast_to(rstd, (16, 128))
                r.n2[rows, :] = jnp.where(real(i), hat * gain + shift, 0.0).astype(bf16)
            return 0

        blocks_of(13, 16, second_norm, group=3)
        r.n2t[...] = r.n2[...].T

    def forward(j):
        slot = remainder(j, 2)
        wait(weights(j))

        @pl.when(j + 1 < CHUNKS)
        def _():
            start(weights(j + 1))

        columns = pl.ds(pl.multiple_of(j * WIDTH, WIDTH), WIDTH)
        for b in range(WIDTH // 256):
            part = slice(256 * b, 256 * (b + 1))
            hid[:ROWS, part] = jnp.dot(r.n2[:ROWS, :], r.w_in[slot, :, part], preferred_element_type=f32)
            dact[:ROWS, part] = jnp.dot(r.cots[:ROWS, :], r.w_out[slot, :, part], preferred_element_type=f32)
        shift = bias2[:, columns]

        def rows(at, i, total):
            value, slope = gelu_parts(hid[at, :] + shift)
            act[at, :] = value.astype(bf16)
            d = (dact[at, :] * slope).astype(bf16)
            dhid[at, :] = d
            return total + jnp.sum(d.astype(f32).reshape(4, 8, WIDTH), axis=0)

        total = blocks_of(ROWS // 32, 32, rows, jnp.zeros((8, WIDTH), f32))
        early[pl.ds(j, 1), :WIDTH] = jnp.sum(total, axis=0, keepdims=True)

    def gradients(j):
        slot = remainder(j, 2)

        def rows(at, i, _):
            out = jnp.dot(r.cott[at, :], act[...], preferred_element_type=f32).reshape(2, 4, 2, 2, 8, WIDTH)
            r.own[0][i] = out[..., :384]
            r.own[1][i, :, :, :, :, :, :128] = out[..., 384:]
            inn = jnp.dot(r.n2t[at, :], dhid[...], preferred_element_type=f32).reshape(2, 4, 2, 2, 8, WIDTH)
            r.own[1][i, :, :, :, :, :, 128:] = inn[..., :256]
            r.own[2][i] = inn[..., 256:]
            return 0

        blocks_of(4, 256, rows)
        start(pair_copies(j))
        for b in range(4):
            part = slice(256 * b, 256 * (b + 1))
            dn2[:, part] += lax.dot_general(
                dhid[:ROWS, :],
                r.w_in[slot, part, :],
                (((1,), (1,)), ((), ())),
                preferred_element_type=f32,
            )

    def across(a, b):
        return lax.dot_general(a, b, (((1,), (1,)), ((), ())), preferred_element_type=f32)

    def fold_into(ref, row, lane, total):
        summed = jnp.sum(total, axis=0, keepdims=True)
        for k in range(4):
            ref[row + k : row + k + 1, lane : lane + 256] += summed[:, 256 * k : 256 * (k + 1)]

    def token_backward(b):
        gain = gain2[...]
        for half in range(2):
            dmr(b, half)[IMAGE:, :] = jnp.zeros((256 - IMAGE, 512), bf16)

        def second_norm(at, i, sums):
            rows = rows_of(b, i)
            hat, incoming = r.hat2[rows, :], dn2[rows, :]
            g = r.cots[rows, :].astype(f32)
            dmixed = g + norm_backward(incoming, hat, r.rstd2[rows, :1], gain)
            dn2[rows, :] = dmixed
            rounded = dmixed.astype(bf16)
            for half in range(2):
                dmr(b, half)[at, :] = rounded[:, columns_of(half)]
            r.columns[at, :] += jnp.broadcast_to(jnp.sum(dmixed, axis=1, keepdims=True), (16, 128))
            return (sums[0] + folded(incoming * hat), sums[1] + folded(incoming), sums[2] + folded(g))

        zero = jnp.zeros((8, 1024), f32)
        sums = blocks_of(13, 16, second_norm, (zero, zero, zero), group=2)
        fold_into(early, 0, 512, sums[0])
        fold_into(early, 4, 512, sums[1])
        fold_into(early, 0, 768, sums[2])
        for half in range(2):
            token_hidden(b, columns_of(half))
            dact[...] = jnp.dot(r.tout[...], dmr(b, half)[...], preferred_element_type=f32)

            def back(at, i, _):
                slope = gelu_parts(hid[at, :] + r.bias1[at, :1])[1]
                dh1(b, half)[at, :] = (dact[at, :] * slope).astype(bf16)
                return 0

            blocks_of(16, 32, back)

    def token_gradients(b):
        ones = jnp.ones((8, 512), bf16)
        for half in range(2):
            columns = columns_of(half)
            r.grad_tin[...] += across(dh1(b, half)[...], r.n1[b, :, columns])
            r.grad_tout[...] += across(r.act1[b, :, columns], dmr(b, half)[...])
            total = across(ones, dh1(b, half)[...])[:1]
            for k in range(4):
                late[k : k + 1, 256:] += total[:, 128 * k : 128 * (k + 1)]

    def send_token_gradients():
        for h, grad in enumerate((r.grad_tin, r.grad_tout)):
            r.own[2][:, :, :, :, h] = grad[...].reshape(4, 2, 4, 2, 8, 256)
        start(pair_copies(CHUNKS))

    def input_gradients(b):
        gain = gain1[...]
        for half in range(2):
            r.hat2[:IMAGE, columns_of(half)] = jnp.dot(
                r.tint[:IMAGE, :], dh1(b, half)[...], preferred_element_type=f32
            )

        def first_norm(at, i, sums):
            hat, rstd = standardized(r.xs[b, at, :].astype(f32))
            incoming = r.hat2[at, :]
            rows = rows_of(b, i)
            dn2[rows, :] += norm_backward(incoming, hat, rstd, gain)
            return (sums[0] + folded(incoming * hat), sums[1] + folded(incoming))

        zero = jnp.zeros((8, 1024), f32)
        sums = blocks_of(13, 16, first_norm, (zero, zero), group=2)
        fold_into(late, 0, 0, sums[0])
        fold_into(late, 4, 0, sums[1])

    def interleave():
        def rows(at, i, _):
            both = [dn2[pl.ds(pl.multiple_of(IMAGE * b + 8 * i, 8), 8), :] for b in range(2)]
            grad_inputs[pl.ds(pl.multiple_of(8 * i, 8), 8)] = jnp.stack(both, axis=1).astype(bf16)
            return 0

        blocks_of(24, 8, rows)
        both = [dn2[IMAGE * b + 192 : IMAGE * b + 200, :][: PATCHES - 192] for b in range(2)]
        grad_inputs[192:PATCHES] = jnp.stack(both, axis=1).astype(bf16)

    def sums_copies(which, step):
        at = (r.early, r.late)[which]
        send, recv = r.sums_send.at[which, step], r.sums_recv.at[which, step]
        if step == 0:
            return [remote(at[0], at[1], send.at[0], recv.at[0], device(core=1 - core))]
        axis, ring = AXES[step - 1], at[step + 1]
        return [
            remote(ring.at[0], ring.at[by], send.at[by - 1], recv.at[by - 1], device(**{axis: along(axis, by)}))
            for by in (1, 2, 3)
        ]

    def sums_stage(which, step):
        at = (r.early, r.late)[which]
        if step == 0:
            start(sums_copies(which, 0))
            return None
        wait(sums_copies(which, step - 1))
        if step == 1:
            total = at[0][...] + at[1][...]
        else:
            ring, mine = at[step], me[AXES[step - 2]]
            terms = [ring[remainder(mine + 4 - k, 4)] for k in range(4)]
            total = (terms[0] + terms[1]) + (terms[2] + terms[3])
        if step < 4:
            at[step + 1][0] = total
            start(sums_copies(which, step))
        return total

    def unfold(total, row, lane):
        return [total[row + k : row + k + 1, lane : lane + 256] for k in range(4)]

    def finish_early(total):
        for j in range(CHUNKS):
            grad_b2[:, WIDTH * j : WIDTH * (j + 1)] = total[j : j + 1, :WIDTH]
        for n, (row, lane) in ((2, (0, 512)), (3, (4, 512)), (4, (0, 768))):
            for k, part in enumerate(unfold(total, row, lane)):
                grad_norms[n : n + 1, 256 * k : 256 * (k + 1)] = part
        grad_bo[...] = total[4:5, 768 : 768 + PATCHES]

    def finish_late(total):
        for n, row in ((0, 0), (1, 4)):
            for k, part in enumerate(unfold(total, row, 0)):
                grad_norms[n : n + 1, 256 * k : 256 * (k + 1)] = part
        for k in range(4):
            grad_b1[:, 128 * k : 128 * (k + 1)] = total[k : k + 1, 256:]

    start(weights(jnp.int32(0)))
    for ref in (act, dhid):
        ref[ROWS:, :] = jnp.zeros((512 - ROWS, WIDTH), bf16)
    for ref in (dn2, early, late, r.columns, r.grad_tin, r.grad_tout):
        ref[...] = jnp.zeros(ref.shape, f32)
    prologue()
    pl.semaphore_wait(barrier, len(partners))

    def slot_of(t, _):
        @pl.when(t < CHUNKS)
        def _():
            forward(t)

        @pl.when((t >= 1) & (t <= CHUNKS))
        def _():
            stage(1, t - 1)

        @pl.when(t < CHUNKS)
        def _():
            gradients(t)

        @pl.when((t >= CHUNKS) & (t < CHUNKS + 2))
        def _():
            token_backward(t - CHUNKS)

        @pl.when((t >= CHUNKS + 2) & (t < CHUNKS + 4))
        def _():
            token_gradients(t - CHUNKS - 2)

        @pl.when(t == CHUNKS + 3)
        def _():
            send_token_gradients()

        @pl.when(t == CHUNKS + 4)
        def _():
            stage(1, CHUNKS)

        @pl.when((t >= CHUNKS + 4) & (t < CHUNKS + 6))
        def _():
            input_gradients(t - CHUNKS - 4)

        @pl.when(t == EARLY_SUMS)
        def _():
            early[4:5, 768:] = r.columns[...].T[:1, :]

        for step in range(4):
            for which, first in enumerate((EARLY_SUMS, LATE_SUMS)):

                @pl.when(t == first + step)
                def _():
                    sums_stage(which, step)

        serve(t)

        @pl.when(t == LATE_SUMS + 1)
        def _():
            interleave()

        return 0

    lax.fori_loop(0, SLOTS, slot_of, 0)
    finish_early(sums_stage(0, 4))
    finish_late(sums_stage(1, 4))
    for h in range(2):
        for j in range(CHUNKS):
            for g, out in enumerate((grad_out, grad_in)):
                out[8 * h : 8 * (h + 1), WIDTH * j : WIDTH * (j + 1)] = r.done[
                    h, j, :, WIDTH * g : WIDTH * (g + 1)
                ]
    grad_tin[...] = r.done_token[0, :, :PATCHES]
    grad_tout[...] = r.done_token[1, :, :PATCHES]


def hand_over(*refs):
    count = len(refs) // 2
    for source, target in zip(refs[:count], refs[count:]):
        target[...] = source[...]


def per_device(
    inputs,
    cotangent,
    first_gain,
    first_shift,
    token_in,
    token_in_bias,
    token_out,
    second_gain,
    second_shift,
    channel_in,
    channel_in_bias,
    channel_out,
):
    f32 = jnp.float32
    hidden = channel_in.shape[1]
    vmem, anywhere = pl.BlockSpec(memory_space=pltpu.VMEM), pl.BlockSpec(memory_space=pl.ANY)

    results = pl.pallas_call(
        block_kernel,
        out_shape=(
            jax.ShapeDtypeStruct((PATCHES, 2, 1024), jnp.bfloat16),
            jax.ShapeDtypeStruct((8, PATCHES), f32),
            jax.ShapeDtypeStruct((8, PATCHES), f32),
            jax.ShapeDtypeStruct((16, hidden), f32),
            jax.ShapeDtypeStruct((16, hidden), f32),
            jax.ShapeDtypeStruct((5, 1024), f32),
            jax.ShapeDtypeStruct((1, 512), f32),
            jax.ShapeDtypeStruct((1, PATCHES), f32),
            jax.ShapeDtypeStruct((1, hidden), f32),
        ),
        in_specs=[vmem] * 9 + [anywhere, vmem, anywhere],
        out_specs=(vmem,) * 9,
        scratch_shapes=(scratch_of(),),
        compiler_params=pltpu.CompilerParams(collective_id=0, has_side_effects=True, vmem_limit_bytes=67_000_000),
        name="block_backward",
    )(
        inputs.swapaxes(0, 1),
        cotangent.swapaxes(0, 1),
        first_gain.reshape(1, -1),
        first_shift.reshape(1, -1),
        token_in.T,
        token_in_bias.reshape(1, -1),
        token_out.T,
        second_gain.reshape(1, -1),
        second_shift.reshape(1, -1),
        channel_in,
        channel_in_bias.reshape(1, -1),
        channel_out,
    )
    results = pl.pallas_call(
        hand_over,
        out_shape=tuple(jax.ShapeDtypeStruct(a.shape, a.dtype) for a in results),
        in_specs=[vmem] * 9,
        out_specs=(vmem,) * 9,
        name="hand_over",
    )(*results)
    return (results[0].swapaxes(0, 1), *results[1:6], *(a[0] for a in results[6:]))


def solution(mesh):
    split = Mesh(
        mesh.devices.reshape(mesh.shape["grp"], 4, 2, 4, 2),
        ("grp", "dev_0", "dev_1", "dev_2", "dev_3"),
    )
    in_specs = (
        P(GRP_DEV, None, None),
        P(GRP_DEV, None, None),
        P(),
        P(),
        P(),
        P(),
        P(),
        P(),
        P(),
        P(),
        P(),
        P(),
    )
    out_specs = (
        P(GRP_DEV, None, None),
        P(DEV, None),
        P(DEV, None),
        P(DEV, None),
        P(DEV, None),
        P(),
        P(),
        P(),
        P(),
    )
    return jax.shard_map(
        per_device, mesh=split, in_specs=in_specs, out_specs=out_specs, check_vma=False
    )
```

time: 157 us -> 152 us (0.968)
  local copies, waits for them, and re-layouts: 23.5 us -> 0 us
  Pallas kernels: 132 us -> 151 us
    unnamed x13 -> x0, local copies, waits for them, and re-layouts: 22 us -> none
    pallas_call x1 -> x2, Pallas kernels: 132 us -> 151 us  [the longest x1 148 us: per_device(): pl.pallas_call(block_kernel, out_shape=(jax.ShapeDtypeStruct((PATCHES, 2,...]
where the time goes in v3:
time: 152 us
  Pallas kernels  151 us (99%)
    pallas_call x1, Pallas kernels, per_device(): pl.pallas_call(block_kernel, out_shape=(jax.ShapeDtypeStruct((PATCHES, 2,...  148 us

profile of v3, /device:TPU:0, one launch (start us, length us, event | category | flops | bytes accessed | tf_op | source)
XLA Modules:
  0.0 151.5 jit_solution(10227378214200263833)
XLA Ops:
  0.6 148.4 %block_backward.1 = (bf16[196,2,1024]{2,1,0:T(2,128)(2,1)}, f32[8,196]{1,0:T(8,128)}, f32[8,196]{1,0:T(8,128)}, f32[16,4096]{1,0:T(8,128)}, f32[16,4096]{1,0:T(8...) custom-call(bf16[196,2,1024]{2,1,0:T(2,128)(2,1)} %bitcast.14, ...), custom_call_target="tpu_custom_call" | custom-call | tf_op jit(solution)/shard_map/block_backward/pallas_call | solution.py:754
  149.0 2.5 %hand_over.1 = (bf16[196,2,1024]{2,1,0:T(2,128)(2,1)}, f32[8,196]{1,0:T(8,128)}, f32[8,196]{1,0:T(8,128)}, f32[16,4096]{1,0:T(8,128)}, f32[16,4096]{1,0:T(8,128)...) custom-call(bf16[196,2,1024]{2,1,0:T(2,128)(2,1)} %get-tuple-element.27.refs_0_, ...), custom_call_target="tpu_custom_call" | custom-call | tf_op jit(solution)/shard_map/hand_over/pallas_call | solution.py:786

commit v4 on v3

--- a/solution.py
+++ b/solution.py
@@ -23,13 +23,12 @@
 PATCHES = 196
 COLOURS = (("x", "z", "y", 384), ("y", "z", "x", 384), ("z", "x", "y", 256))
 FIRST = (0, 384, 768)
-LAG = (0, 0, 2, 4, 6, 8, 10, 12)
-LATE = 14
-LATE_LAG = (0, 0, 1, 3, 4, 5, 6, 7)
-PIECES = CHUNKS + 6
+LAG = (0, 2, 5, 8, 11, 14, 17, 20)
+AFTER = 2 * CHUNKS
+LATE_SLOT = (0, 20, 22, 25, 27, 29, 32, 34)
 SLOTS = 2 * (CHUNKS - 1) + LAG[-1] + 1
-EARLY_SUMS = CHUNKS + 3
-LATE_SUMS = CHUNKS + 6
+EARLY_SUMS = AFTER + 2
+LATE_SUMS = AFTER + 6
 
 
 def remainder(a, b):
@@ -346,15 +345,15 @@
             wait([both_copy(j)])
 
     def serve(t):
-        for s in range(7, 1, -1):
+        for s in range(7, 0, -1):
             from_start = t - LAG[s]
             j = lax.div(from_start, jnp.int32(2))
 
-            @pl.when((from_start >= 0) & (from_start < 2 * CHUNKS) & (remainder(from_start + 2 * CHUNKS, 2) == 0))
+            @pl.when((from_start >= 0) & (from_start < 2 * CHUNKS) & (remainder(from_start + 4 * CHUNKS, 2) == 0))
             def _():
                 stage(s, j)
 
-            @pl.when(t == LATE + LATE_LAG[s])
+            @pl.when(t == LATE_SLOT[s])
             def _():
                 stage(s, CHUNKS)
 
@@ -663,37 +662,31 @@
     pl.semaphore_wait(barrier, len(partners))
 
     def slot_of(t, _):
-        @pl.when(t < CHUNKS)
+        chunk = lax.div(t, jnp.int32(2))
+
+        @pl.when((t < AFTER) & (remainder(t, 2) == 0))
         def _():
-            forward(t)
-
-        @pl.when((t >= 1) & (t <= CHUNKS))
+            forward(chunk)
+
+        @pl.when((t < AFTER) & (remainder(t, 2) == 1))
         def _():
-            stage(1, t - 1)
-
-        @pl.when(t < CHUNKS)
+            gradients(chunk)
+
+        @pl.when((t >= AFTER) & (t < AFTER + 2))
         def _():
-            gradients(t)
-
-        @pl.when((t >= CHUNKS) & (t < CHUNKS + 2))
+            token_backward(t - AFTER)
+
+        @pl.when((t >= AFTER + 2) & (t < AFTER + 4))
         def _():
-            token_backward(t - CHUNKS)
-
-        @pl.when((t >= CHUNKS + 2) & (t < CHUNKS + 4))
-        def _():
-            token_gradients(t - CHUNKS - 2)
-
-        @pl.when(t == CHUNKS + 3)
+            token_gradients(t - AFTER - 2)
+
+        @pl.when(t == AFTER + 3)
         def _():
             send_token_gradients()
 
-        @pl.when(t == CHUNKS + 4)
+        @pl.when((t >= AFTER + 4) & (t < AFTER + 6))
         def _():
-            stage(1, CHUNKS)
-
-        @pl.when((t >= CHUNKS + 4) & (t < CHUNKS + 6))
-        def _():
-            input_gradients(t - CHUNKS - 4)
+            input_gradients(t - AFTER - 4)
 
         @pl.when(t == EARLY_SUMS)
         def _():

time: 152 us -> 134 us (0.88)
  Pallas kernels: 151 us -> 134 us
    pallas_call x1, Pallas kernels: 148 us -> 131 us  [per_device(): pl.pallas_call(block_kernel, out_shape=(jax.ShapeDtypeStruct((PATCHES, 2,...]
where the time goes in v4:
time: 134 us
  Pallas kernels  134 us (100%)
    pallas_call x1, Pallas kernels, per_device(): pl.pallas_call(block_kernel, out_shape=(jax.ShapeDtypeStruct((PATCHES, 2,...  131 us

profile of v4, /device:TPU:0, one launch (start us, length us, event | category | flops | bytes accessed | tf_op | source)
XLA Modules:
  0.0 134.2 jit_solution(13708066902419229006)
XLA Ops:
  0.6 131.1 %block_backward.1 = (bf16[196,2,1024]{2,1,0:T(2,128)(2,1)}, f32[8,196]{1,0:T(8,128)}, f32[8,196]{1,0:T(8,128)}, f32[16,4096]{1,0:T(8,128)}, f32[16,4096]{1,0:T(8...) custom-call(bf16[196,2,1024]{2,1,0:T(2,128)(2,1)} %bitcast.14, ...), custom_call_target="tpu_custom_call" | custom-call | tf_op jit(solution)/shard_map/block_backward/pallas_call | solution.py:747
  131.7 2.5 %hand_over.1 = (bf16[196,2,1024]{2,1,0:T(2,128)(2,1)}, f32[8,196]{1,0:T(8,128)}, f32[8,196]{1,0:T(8,128)}, f32[16,4096]{1,0:T(8,128)}, f32[16,4096]{1,0:T(8,128)...) custom-call(bf16[196,2,1024]{2,1,0:T(2,128)(2,1)} %get-tuple-element.27.refs_0_, ...), custom_call_target="tpu_custom_call" | custom-call | tf_op jit(solution)/shard_map/hand_over/pallas_call | solution.py:779

commit v5 on v4

--- a/solution.py
+++ b/solution.py
@@ -453,7 +453,7 @@
                     r.act1[b, at, columns] = value.astype(bf16)
                     return 0
 
-                blocks_of(16, 32, activate, group=2)
+                blocks_of(16, 32, activate, group=4)
             for half in range(2):
                 columns = columns_of(half)
                 r.hat2[IMAGE * b : IMAGE * (b + 1), columns] = jnp.dot(
@@ -496,7 +496,7 @@
             dhid[at, :] = d
             return total + jnp.sum(d.astype(f32).reshape(4, 8, WIDTH), axis=0)
 
-        total = blocks_of(ROWS // 32, 32, rows, jnp.zeros((8, WIDTH), f32))
+        total = blocks_of(ROWS // 32, 32, rows, jnp.zeros((8, WIDTH), f32), group=2)
         early[pl.ds(j, 1), :WIDTH] = jnp.sum(total, axis=0, keepdims=True)
 
     def gradients(j):
@@ -561,7 +561,7 @@
                 dh1(b, half)[at, :] = (dact[at, :] * slope).astype(bf16)
                 return 0
 
-            blocks_of(16, 32, back)
+            blocks_of(16, 32, back, group=4)
 
     def token_gradients(b):
         ones = jnp.ones((8, 512), bf16)

time: 134 us -> 131 us (0.978)
  Pallas kernels: 134 us -> 130 us
    pallas_call x1, Pallas kernels: 131 us -> 128 us  [per_device(): pl.pallas_call(block_kernel, out_shape=(jax.ShapeDtypeStruct((PATCHES, 2,...]
where the time goes in v5:
time: 131 us
  Pallas kernels  130 us (99%)
    pallas_call x1, Pallas kernels, per_device(): pl.pallas_call(block_kernel, out_shape=(jax.ShapeDtypeStruct((PATCHES, 2,...  128 us

profile of v5, /device:TPU:0, one launch (start us, length us, event | category | flops | bytes accessed | tf_op | source)
XLA Modules:
  0.0 131.1 jit_solution(6610245831866091099)
XLA Ops:
  0.6 127.9 %block_backward.1 = (bf16[196,2,1024]{2,1,0:T(2,128)(2,1)}, f32[8,196]{1,0:T(8,128)}, f32[8,196]{1,0:T(8,128)}, f32[16,4096]{1,0:T(8,128)}, f32[16,4096]{1,0:T(8...) custom-call(bf16[196,2,1024]{2,1,0:T(2,128)(2,1)} %bitcast.14, ...), custom_call_target="tpu_custom_call" | custom-call | tf_op jit(solution)/shard_map/block_backward/pallas_call | solution.py:747
  128.6 2.5 %hand_over.1 = (bf16[196,2,1024]{2,1,0:T(2,128)(2,1)}, f32[8,196]{1,0:T(8,128)}, f32[8,196]{1,0:T(8,128)}, f32[16,4096]{1,0:T(8,128)}, f32[16,4096]{1,0:T(8,128)...) custom-call(bf16[196,2,1024]{2,1,0:T(2,128)(2,1)} %get-tuple-element.27.refs_0_, ...), custom_call_target="tpu_custom_call" | custom-call | tf_op jit(solution)/shard_map/hand_over/pallas_call | solution.py:779
